TPU v7x, 32 devices: a 4x4x1 block of a 4x4x8 slice. The times are simulated.
32 devices in a mesh: parts: 1 (over z), data: 32 (over y, x, core).
Axes of the slice: x: 4, y: 4, z: 1, core: 2. Of those that a mesh axis runs over, the one named last changes fastest.
The devices are a block of a 4x4x8 slice.
Arguments:
- feat_rows: bfloat16 [131072, 54], P('data')
- labels: int32 [131072], P('data')
- pos_init: float32 [54, 128], P(None, 'parts')
- mom_init: float32 [54, 128], P(None, 'parts')
- step_sizes: float32 [64, 128], P(None, 'parts')
Outputs:
- output 1: float32 [54, 128], P(None, 'parts')
- output 2: float32 [54, 128], P(None, 'parts')
- output 3: float32 [64, 128], P(None, 'parts')
All inputs are finite; a program needn't handle non-finite values.
Results may differ from a plain program's by a relative error of at most 0.001.
Values are sent between devices in bfloat16 or wider.
A program may use at most 768 MiB of HBM per device.

v0:
```python
import jax
import jax.numpy as jnp
from jax import lax
from jax.sharding import PartitionSpec as P

PRIOR_VAR = 4.0


def solution(mesh):
    row_spec = P("data", None)
    chain_spec = P(None, "parts")

    def local_chains(feat_rows, labels, pos_init, mom_init, step_sizes):
        label_col = labels.astype(jnp.float32)[:, None]

        def gradient_at(positions):
            logits = jnp.dot(feat_rows, positions.astype(jnp.bfloat16), preferred_element_type=jnp.float32)
            residual = (label_col - jax.nn.sigmoid(logits)).astype(jnp.bfloat16)
            grad_part = lax.dot_general(feat_rows, residual, (((0,), (0,)), ((), ())), preferred_element_type=jnp.float32)
            gradient = lax.psum(grad_part, "data") - positions / PRIOR_VAR
            return gradient, logits

        grad_init, _ = gradient_at(pos_init)

        def leap_step(loop_state, step_size):
            positions, momentum, gradient = loop_state
            momentum = momentum + 0.5 * step_size * gradient
            positions = positions + step_size * momentum
            gradient, logits = gradient_at(positions)
            momentum = momentum + 0.5 * step_size * gradient
            loss_part = jnp.sum(jax.nn.softplus(logits) - label_col * logits, axis=0)
            potential = lax.psum(loss_part, "data") + jnp.sum(positions * positions, axis=0) / (2.0 * PRIOR_VAR)
            energy = potential + 0.5 * jnp.sum(momentum * momentum, axis=0)
            return (positions, momentum, gradient), energy

        (positions, momentum, _), energies = lax.scan(leap_step, (pos_init, mom_init, grad_init), step_sizes)
        return positions, momentum, energies

    return jax.shard_map(local_chains, mesh=mesh, in_specs=(row_spec, P("data"), chain_spec, chain_spec, chain_spec), out_specs=(chain_spec, chain_spec, chain_spec), check_vma=False)
```

profile of v0, /device:TPU:97, one launch (start us, length us, event | category | flops | bytes accessed | tf_op | source)
XLA Modules:
  0.0 3211.4 jit_solution(432108307467294079)
XLA Ops:
  4.4 50.1 %psum.21 = f32[54,128]{1,0:T(8,128)S(1)} all-reduce(f32[54,128]{1,0:T(8,128)S(1)} %fusion.11), channel_id=1, replica_groups=mesh['parts'=1,'data'=32] {'data'}, use_global_device_ids=true, to_apply=%region_0.0 | all-reduce | flops 6912 | bytes 55296 | tf_op jit(solution)/shard_map/psum | solution.py:20
  54.5 3156.3 %while.16 = (s32[]{:T(128)}, f32[54,128]{1,0:T(8,128)S(1)}, f32[54,128]{1,0:T(8,128)S(1)}, f32[54,128]{1,0:T(8,128)S(1)}, f32[64,128]{1,0:T(8,128)}, /*index=5*/...) while((s32[]{:T(128)}, f32[54,128]{1,0:T(8,128)S(1)}, ...), condition=%wide.region_7.8_spmd, body=%wide.region_1.7_spmd.sunk | while | flops 120697216 | bytes 5507693 | solution.py:36
  155.2 44.8 %all-reduce.2 = (f32[54,128]{1,0:T(8,128)S(1)}, f32[128]{0:T(128)S(1)}) all-reduce(f32[54,128]{1,0:T(8,128)S(1)} %convolution_bitcast_fusion.3, f32[128]{0:T(128)S(1)} %get-tuple-element.141), channel_id=1, replica_groups=mesh['parts'=1,'data'=32] {'data'}, use_global_device_ids=true, to_apply=%region_2.2 | all-reduce | flops 7040 | bytes 56320 | tf_op jit(solution)/shard_map/while/body/eval_jaxpr/psum | solution.py:20
  204.5 44.8 %all-reduce.2 = (f32[54,128]{1,0:T(8,128)S(1)}, f32[128]{0:T(128)S(1)}) all-reduce(f32[54,128]{1,0:T(8,128)S(1)} %convolution_bitcast_fusion.3, f32[128]{0:T(128)S(1)} %get-tuple-element.141), channel_id=1, replica_groups=mesh['parts'=1,'data'=32] {'data'}, use_global_device_ids=true, to_apply=%region_2.2 | all-reduce | flops 7040 | bytes 56320 | tf_op jit(solution)/shard_map/while/body/eval_jaxpr/psum | solution.py:20
  253.9 44.8 %all-reduce.2 = (f32[54,128]{1,0:T(8,128)S(1)}, f32[128]{0:T(128)S(1)}) all-reduce(f32[54,128]{1,0:T(8,128)S(1)} %convolution_bitcast_fusion.3, f32[128]{0:T(128)S(1)} %get-tuple-element.141), channel_id=1, replica_groups=mesh['parts'=1,'data'=32] {'data'}, use_global_device_ids=true, to_apply=%region_2.2 | all-reduce | flops 7040 | bytes 56320 | tf_op jit(solution)/shard_map/while/body/eval_jaxpr/psum | solution.py:20
  303.2 44.8 %all-reduce.2 = (f32[54,128]{1,0:T(8,128)S(1)}, f32[128]{0:T(128)S(1)}) all-reduce(f32[54,128]{1,0:T(8,128)S(1)} %convolution_bitcast_fusion.3, f32[128]{0:T(128)S(1)} %get-tuple-element.141), channel_id=1, replica_groups=mesh['parts'=1,'data'=32] {'data'}, use_global_device_ids=true, to_apply=%region_2.2 | all-reduce | flops 7040 | bytes 56320 | tf_op jit(solution)/shard_map/while/body/eval_jaxpr/psum | solution.py:20
  352.5 44.8 %all-reduce.2 = (f32[54,128]{1,0:T(8,128)S(1)}, f32[128]{0:T(128)S(1)}) all-reduce(f32[54,128]{1,0:T(8,128)S(1)} %convolution_bitcast_fusion.3, f32[128]{0:T(128)S(1)} %get-tuple-element.141), channel_id=1, replica_groups=mesh['parts'=1,'data'=32] {'data'}, use_global_device_ids=true, to_apply=%region_2.2 | all-reduce | flops 7040 | bytes 56320 | tf_op jit(solution)/shard_map/while/body/eval_jaxpr/psum | solution.py:20
  401.9 44.8 %all-reduce.2 = (f32[54,128]{1,0:T(8,128)S(1)}, f32[128]{0:T(128)S(1)}) all-reduce(f32[54,128]{1,0:T(8,128)S(1)} %convolution_bitcast_fusion.3, f32[128]{0:T(128)S(1)} %get-tuple-element.141), channel_id=1, replica_groups=mesh['parts'=1,'data'=32] {'data'}, use_global_device_ids=true, to_apply=%region_2.2 | all-reduce | flops 7040 | bytes 56320 | tf_op jit(solution)/shard_map/while/body/eval_jaxpr/psum | solution.py:20
  451.2 44.8 %all-reduce.2 = (f32[54,128]{1,0:T(8,128)S(1)}, f32[128]{0:T(128)S(1)}) all-reduce(f32[54,128]{1,0:T(8,128)S(1)} %convolution_bitcast_fusion.3, f32[128]{0:T(128)S(1)} %get-tuple-element.141), channel_id=1, replica_groups=mesh['parts'=1,'data'=32] {'data'}, use_global_device_ids=true, to_apply=%region_2.2 | all-reduce | flops 7040 | bytes 56320 | tf_op jit(solution)/shard_map/while/body/eval_jaxpr/psum | solution.py:20
  500.5 44.8 %all-reduce.2 = (f32[54,128]{1,0:T(8,128)S(1)}, f32[128]{0:T(128)S(1)}) all-reduce(f32[54,128]{1,0:T(8,128)S(1)} %convolution_bitcast_fusion.3, f32[128]{0:T(128)S(1)} %get-tuple-element.141), channel_id=1, replica_groups=mesh['parts'=1,'data'=32] {'data'}, use_global_device_ids=true, to_apply=%region_2.2 | all-reduce | flops 7040 | bytes 56320 | tf_op jit(solution)/shard_map/while/body/eval_jaxpr/psum | solution.py:20
  549.9 44.8 %all-reduce.2 = (f32[54,128]{1,0:T(8,128)S(1)}, f32[128]{0:T(128)S(1)}) all-reduce(f32[54,128]{1,0:T(8,128)S(1)} %convolution_bitcast_fusion.3, f32[128]{0:T(128)S(1)} %get-tuple-element.141), channel_id=1, replica_groups=mesh['parts'=1,'data'=32] {'data'}, use_global_device_ids=true, to_apply=%region_2.2 | all-reduce | flops 7040 | bytes 56320 | tf_op jit(solution)/shard_map/while/body/eval_jaxpr/psum | solution.py:20
  599.2 44.8 %all-reduce.2 = (f32[54,128]{1,0:T(8,128)S(1)}, f32[128]{0:T(128)S(1)}) all-reduce(f32[54,128]{1,0:T(8,128)S(1)} %convolution_bitcast_fusion.3, f32[128]{0:T(128)S(1)} %get-tuple-element.141), channel_id=1, replica_groups=mesh['parts'=1,'data'=32] {'data'}, use_global_device_ids=true, to_apply=%region_2.2 | all-reduce | flops 7040 | bytes 56320 | tf_op jit(solution)/shard_map/while/body/eval_jaxpr/psum | solution.py:20
  648.5 44.8 %all-reduce.2 = (f32[54,128]{1,0:T(8,128)S(1)}, f32[128]{0:T(128)S(1)}) all-reduce(f32[54,128]{1,0:T(8,128)S(1)} %convolution_bitcast_fusion.3, f32[128]{0:T(128)S(1)} %get-tuple-element.141), channel_id=1, replica_groups=mesh['parts'=1,'data'=32] {'data'}, use_global_device_ids=true, to_apply=%region_2.2 | all-reduce | flops 7040 | bytes 56320 | tf_op jit(solution)/shard_map/while/body/eval_jaxpr/psum | solution.py:20
  697.9 44.8 %all-reduce.2 = (f32[54,128]{1,0:T(8,128)S(1)}, f32[128]{0:T(128)S(1)}) all-reduce(f32[54,128]{1,0:T(8,128)S(1)} %convolution_bitcast_fusion.3, f32[128]{0:T(128)S(1)} %get-tuple-element.141), channel_id=1, replica_groups=mesh['parts'=1,'data'=32] {'data'}, use_global_device_ids=true, to_apply=%region_2.2 | all-reduce | flops 7040 | bytes 56320 | tf_op jit(solution)/shard_map/while/body/eval_jaxpr/psum | solution.py:20
  747.2 44.8 %all-reduce.2 = (f32[54,128]{1,0:T(8,128)S(1)}, f32[128]{0:T(128)S(1)}) all-reduce(f32[54,128]{1,0:T(8,128)S(1)} %convolution_bitcast_fusion.3, f32[128]{0:T(128)S(1)} %get-tuple-element.141), channel_id=1, replica_groups=mesh['parts'=1,'data'=32] {'data'}, use_global_device_ids=true, to_apply=%region_2.2 | all-reduce | flops 7040 | bytes 56320 | tf_op jit(solution)/shard_map/while/body/eval_jaxpr/psum | solution.py:20
  796.5 44.8 %all-reduce.2 = (f32[54,128]{1,0:T(8,128)S(1)}, f32[128]{0:T(128)S(1)}) all-reduce(f32[54,128]{1,0:T(8,128)S(1)} %convolution_bitcast_fusion.3, f32[128]{0:T(128)S(1)} %get-tuple-element.141), channel_id=1, replica_groups=mesh['parts'=1,'data'=32] {'data'}, use_global_device_ids=true, to_apply=%region_2.2 | all-reduce | flops 7040 | bytes 56320 | tf_op jit(solution)/shard_map/while/body/eval_jaxpr/psum | solution.py:20
  845.9 44.8 %all-reduce.2 = (f32[54,128]{1,0:T(8,128)S(1)}, f32[128]{0:T(128)S(1)}) all-reduce(f32[54,128]{1,0:T(8,128)S(1)} %convolution_bitcast_fusion.3, f32[128]{0:T(128)S(1)} %get-tuple-element.141), channel_id=1, replica_groups=mesh['parts'=1,'data'=32] {'data'}, use_global_device_ids=true, to_apply=%region_2.2 | all-reduce | flops 7040 | bytes 56320 | tf_op jit(solution)/shard_map/while/body/eval_jaxpr/psum | solution.py:20
  895.2 44.8 %all-reduce.2 = (f32[54,128]{1,0:T(8,128)S(1)}, f32[128]{0:T(128)S(1)}) all-reduce(f32[54,128]{1,0:T(8,128)S(1)} %convolution_bitcast_fusion.3, f32[128]{0:T(128)S(1)} %get-tuple-element.141), channel_id=1, replica_groups=mesh['parts'=1,'data'=32] {'data'}, use_global_device_ids=true, to_apply=%region_2.2 | all-reduce | flops 7040 | bytes 56320 | tf_op jit(solution)/shard_map/while/body/eval_jaxpr/psum | solution.py:20
  944.5 44.8 %all-reduce.2 = (f32[54,128]{1,0:T(8,128)S(1)}, f32[128]{0:T(128)S(1)}) all-reduce(f32[54,128]{1,0:T(8,128)S(1)} %convolution_bitcast_fusion.3, f32[128]{0:T(128)S(1)} %get-tuple-element.141), channel_id=1, replica_groups=mesh['parts'=1,'data'=32] {'data'}, use_global_device_ids=true, to_apply=%region_2.2 | all-reduce | flops 7040 | bytes 56320 | tf_op jit(solution)/shard_map/while/body/eval_jaxpr/psum | solution.py:20
  993.9 44.8 %all-reduce.2 = (f32[54,128]{1,0:T(8,128)S(1)}, f32[128]{0:T(128)S(1)}) all-reduce(f32[54,128]{1,0:T(8,128)S(1)} %convolution_bitcast_fusion.3, f32[128]{0:T(128)S(1)} %get-tuple-element.141), channel_id=1, replica_groups=mesh['parts'=1,'data'=32] {'data'}, use_global_device_ids=true, to_apply=%region_2.2 | all-reduce | flops 7040 | bytes 56320 | tf_op jit(solution)/shard_map/while/body/eval_jaxpr/psum | solution.py:20
  1043.2 44.8 %all-reduce.2 = (f32[54,128]{1,0:T(8,128)S(1)}, f32[128]{0:T(128)S(1)}) all-reduce(f32[54,128]{1,0:T(8,128)S(1)} %convolution_bitcast_fusion.3, f32[128]{0:T(128)S(1)} %get-tuple-element.141), channel_id=1, replica_groups=mesh['parts'=1,'data'=32] {'data'}, use_global_device_ids=true, to_apply=%region_2.2 | all-reduce | flops 7040 | bytes 56320 | tf_op jit(solution)/shard_map/while/body/eval_jaxpr/psum | solution.py:20
  1092.6 44.8 %all-reduce.2 = (f32[54,128]{1,0:T(8,128)S(1)}, f32[128]{0:T(128)S(1)}) all-reduce(f32[54,128]{1,0:T(8,128)S(1)} %convolution_bitcast_fusion.3, f32[128]{0:T(128)S(1)} %get-tuple-element.141), channel_id=1, replica_groups=mesh['parts'=1,'data'=32] {'data'}, use_global_device_ids=true, to_apply=%region_2.2 | all-reduce | flops 7040 | bytes 56320 | tf_op jit(solution)/shard_map/while/body/eval_jaxpr/psum | solution.py:20
  1141.9 44.8 %all-reduce.2 = (f32[54,128]{1,0:T(8,128)S(1)}, f32[128]{0:T(128)S(1)}) all-reduce(f32[54,128]{1,0:T(8,128)S(1)} %convolution_bitcast_fusion.3, f32[128]{0:T(128)S(1)} %get-tuple-element.141), channel_id=1, replica_groups=mesh['parts'=1,'data'=32] {'data'}, use_global_device_ids=true, to_apply=%region_2.2 | all-reduce | flops 7040 | bytes 56320 | tf_op jit(solution)/shard_map/while/body/eval_jaxpr/psum | solution.py:20
  1191.2 44.8 %all-reduce.2 = (f32[54,128]{1,0:T(8,128)S(1)}, f32[128]{0:T(128)S(1)}) all-reduce(f32[54,128]{1,0:T(8,128)S(1)} %convolution_bitcast_fusion.3, f32[128]{0:T(128)S(1)} %get-tuple-element.141), channel_id=1, replica_groups=mesh['parts'=1,'data'=32] {'data'}, use_global_device_ids=true, to_apply=%region_2.2 | all-reduce | flops 7040 | bytes 56320 | tf_op jit(solution)/shard_map/while/body/eval_jaxpr/psum | solution.py:20
  1240.6 44.8 %all-reduce.2 = (f32[54,128]{1,0:T(8,128)S(1)}, f32[128]{0:T(128)S(1)}) all-reduce(f32[54,128]{1,0:T(8,128)S(1)} %convolution_bitcast_fusion.3, f32[128]{0:T(128)S(1)} %get-tuple-element.141), channel_id=1, replica_groups=mesh['parts'=1,'data'=32] {'data'}, use_global_device_ids=true, to_apply=%region_2.2 | all-reduce | flops 7040 | bytes 56320 | tf_op jit(solution)/shard_map/while/body/eval_jaxpr/psum | solution.py:20
  1289.9 44.8 %all-reduce.2 = (f32[54,128]{1,0:T(8,128)S(1)}, f32[128]{0:T(128)S(1)}) all-reduce(f32[54,128]{1,0:T(8,128)S(1)} %convolution_bitcast_fusion.3, f32[128]{0:T(128)S(1)} %get-tuple-element.141), channel_id=1, replica_groups=mesh['parts'=1,'data'=32] {'data'}, use_global_device_ids=true, to_apply=%region_2.2 | all-reduce | flops 7040 | bytes 56320 | tf_op jit(solution)/shard_map/while/body/eval_jaxpr/psum | solution.py:20
  1339.2 44.8 %all-reduce.2 = (f32[54,128]{1,0:T(8,128)S(1)}, f32[128]{0:T(128)S(1)}) all-reduce(f32[54,128]{1,0:T(8,128)S(1)} %convolution_bitcast_fusion.3, f32[128]{0:T(128)S(1)} %get-tuple-element.141), channel_id=1, replica_groups=mesh['parts'=1,'data'=32] {'data'}, use_global_device_ids=true, to_apply=%region_2.2 | all-reduce | flops 7040 | bytes 56320 | tf_op jit(solution)/shard_map/while/body/eval_jaxpr/psum | solution.py:20
  1388.6 44.8 %all-reduce.2 = (f32[54,128]{1,0:T(8,128)S(1)}, f32[128]{0:T(128)S(1)}) all-reduce(f32[54,128]{1,0:T(8,128)S(1)} %convolution_bitcast_fusion.3, f32[128]{0:T(128)S(1)} %get-tuple-element.141), channel_id=1, replica_groups=mesh['parts'=1,'data'=32] {'data'}, use_global_device_ids=true, to_apply=%region_2.2 | all-reduce | flops 7040 | bytes 56320 | tf_op jit(solution)/shard_map/while/body/eval_jaxpr/psum | solution.py:20
  1437.9 44.8 %all-reduce.2 = (f32[54,128]{1,0:T(8,128)S(1)}, f32[128]{0:T(128)S(1)}) all-reduce(f32[54,128]{1,0:T(8,128)S(1)} %convolution_bitcast_fusion.3, f32[128]{0:T(128)S(1)} %get-tuple-element.141), channel_id=1, replica_groups=mesh['parts'=1,'data'=32] {'data'}, use_global_device_ids=true, to_apply=%region_2.2 | all-reduce | flops 7040 | bytes 56320 | tf_op jit(solution)/shard_map/while/body/eval_jaxpr/psum | solution.py:20
  1487.2 44.8 %all-reduce.2 = (f32[54,128]{1,0:T(8,128)S(1)}, f32[128]{0:T(128)S(1)}) all-reduce(f32[54,128]{1,0:T(8,128)S(1)} %convolution_bitcast_fusion.3, f32[128]{0:T(128)S(1)} %get-tuple-element.141), channel_id=1, replica_groups=mesh['parts'=1,'data'=32] {'data'}, use_global_device_ids=true, to_apply=%region_2.2 | all-reduce | flops 7040 | bytes 56320 | tf_op jit(solution)/shard_map/while/body/eval_jaxpr/psum | solution.py:20
  1536.5 44.8 %all-reduce.2 = (f32[54,128]{1,0:T(8,128)S(1)}, f32[128]{0:T(128)S(1)}) all-reduce(f32[54,128]{1,0:T(8,128)S(1)} %convolution_bitcast_fusion.3, f32[128]{0:T(128)S(1)} %get-tuple-element.141), channel_id=1, replica_groups=mesh['parts'=1,'data'=32] {'data'}, use_global_device_ids=true, to_apply=%region_2.2 | all-reduce | flops 7040 | bytes 56320 | tf_op jit(solution)/shard_map/while/body/eval_jaxpr/psum | solution.py:20
  1585.9 44.8 %all-reduce.2 = (f32[54,128]{1,0:T(8,128)S(1)}, f32[128]{0:T(128)S(1)}) all-reduce(f32[54,128]{1,0:T(8,128)S(1)} %convolution_bitcast_fusion.3, f32[128]{0:T(128)S(1)} %get-tuple-element.141), channel_id=1, replica_groups=mesh['parts'=1,'data'=32] {'data'}, use_global_device_ids=true, to_apply=%region_2.2 | all-reduce | flops 7040 | bytes 56320 | tf_op jit(solution)/shard_map/while/body/eval_jaxpr/psum | solution.py:20
  1635.2 44.8 %all-reduce.2 = (f32[54,128]{1,0:T(8,128)S(1)}, f32[128]{0:T(128)S(1)}) all-reduce(f32[54,128]{1,0:T(8,128)S(1)} %convolution_bitcast_fusion.3, f32[128]{0:T(128)S(1)} %get-tuple-element.141), channel_id=1, replica_groups=mesh['parts'=1,'data'=32] {'data'}, use_global_device_ids=true, to_apply=%region_2.2 | all-reduce | flops 7040 | bytes 56320 | tf_op jit(solution)/shard_map/while/body/eval_jaxpr/psum | solution.py:20
  1684.6 44.8 %all-reduce.2 = (f32[54,128]{1,0:T(8,128)S(1)}, f32[128]{0:T(128)S(1)}) all-reduce(f32[54,128]{1,0:T(8,128)S(1)} %convolution_bitcast_fusion.3, f32[128]{0:T(128)S(1)} %get-tuple-element.141), channel_id=1, replica_groups=mesh['parts'=1,'data'=32] {'data'}, use_global_device_ids=true, to_apply=%region_2.2 | all-reduce | flops 7040 | bytes 56320 | tf_op jit(solution)/shard_map/while/body/eval_jaxpr/psum | solution.py:20
  1733.9 44.8 %all-reduce.2 = (f32[54,128]{1,0:T(8,128)S(1)}, f32[128]{0:T(128)S(1)}) all-reduce(f32[54,128]{1,0:T(8,128)S(1)} %convolution_bitcast_fusion.3, f32[128]{0:T(128)S(1)} %get-tuple-element.141), channel_id=1, replica_groups=mesh['parts'=1,'data'=32] {'data'}, use_global_device_ids=true, to_apply=%region_2.2 | all-reduce | flops 7040 | bytes 56320 | tf_op jit(solution)/shard_map/while/body/eval_jaxpr/psum | solution.py:20
  1783.2 44.8 %all-reduce.2 = (f32[54,128]{1,0:T(8,128)S(1)}, f32[128]{0:T(128)S(1)}) all-reduce(f32[54,128]{1,0:T(8,128)S(1)} %convolution_bitcast_fusion.3, f32[128]{0:T(128)S(1)} %get-tuple-element.141), channel_id=1, replica_groups=mesh['parts'=1,'data'=32] {'data'}, use_global_device_ids=true, to_apply=%region_2.2 | all-reduce | flops 7040 | bytes 56320 | tf_op jit(solution)/shard_map/while/body/eval_jaxpr/psum | solution.py:20
  1832.6 44.8 %all-reduce.2 = (f32[54,128]{1,0:T(8,128)S(1)}, f32[128]{0:T(128)S(1)}) all-reduce(f32[54,128]{1,0:T(8,128)S(1)} %convolution_bitcast_fusion.3, f32[128]{0:T(128)S(1)} %get-tuple-element.141), channel_id=1, replica_groups=mesh['parts'=1,'data'=32] {'data'}, use_global_device_ids=true, to_apply=%region_2.2 | all-reduce | flops 7040 | bytes 56320 | tf_op jit(solution)/shard_map/while/body/eval_jaxpr/psum | solution.py:20
  1881.9 44.8 %all-reduce.2 = (f32[54,128]{1,0:T(8,128)S(1)}, f32[128]{0:T(128)S(1)}) all-reduce(f32[54,128]{1,0:T(8,128)S(1)} %convolution_bitcast_fusion.3, f32[128]{0:T(128)S(1)} %get-tuple-element.141), channel_id=1, replica_groups=mesh['parts'=1,'data'=32] {'data'}, use_global_device_ids=true, to_apply=%region_2.2 | all-reduce | flops 7040 | bytes 56320 | tf_op jit(solution)/shard_map/while/body/eval_jaxpr/psum | solution.py:20
  1931.2 44.8 %all-reduce.2 = (f32[54,128]{1,0:T(8,128)S(1)}, f32[128]{0:T(128)S(1)}) all-reduce(f32[54,128]{1,0:T(8,128)S(1)} %convolution_bitcast_fusion.3, f32[128]{0:T(128)S(1)} %get-tuple-element.141), channel_id=1, replica_groups=mesh['parts'=1,'data'=32] {'data'}, use_global_device_ids=true, to_apply=%region_2.2 | all-reduce | flops 7040 | bytes 56320 | tf_op jit(solution)/shard_map/while/body/eval_jaxpr/psum | solution.py:20
  1980.6 44.8 %all-reduce.2 = (f32[54,128]{1,0:T(8,128)S(1)}, f32[128]{0:T(128)S(1)}) all-reduce(f32[54,128]{1,0:T(8,128)S(1)} %convolution_bitcast_fusion.3, f32[128]{0:T(128)S(1)} %get-tuple-element.141), channel_id=1, replica_groups=mesh['parts'=1,'data'=32] {'data'}, use_global_device_ids=true, to_apply=%region_2.2 | all-reduce | flops 7040 | bytes 56320 | tf_op jit(solution)/shard_map/while/body/eval_jaxpr/psum | solution.py:20
  2029.9 44.8 %all-reduce.2 = (f32[54,128]{1,0:T(8,128)S(1)}, f32[128]{0:T(128)S(1)}) all-reduce(f32[54,128]{1,0:T(8,128)S(1)} %convolution_bitcast_fusion.3, f32[128]{0:T(128)S(1)} %get-tuple-element.141), channel_id=1, replica_groups=mesh['parts'=1,'data'=32] {'data'}, use_global_device_ids=true, to_apply=%region_2.2 | all-reduce | flops 7040 | bytes 56320 | tf_op jit(solution)/shard_map/while/body/eval_jaxpr/psum | solution.py:20
  2079.2 44.8 %all-reduce.2 = (f32[54,128]{1,0:T(8,128)S(1)}, f32[128]{0:T(128)S(1)}) all-reduce(f32[54,128]{1,0:T(8,128)S(1)} %convolution_bitcast_fusion.3, f32[128]{0:T(128)S(1)} %get-tuple-element.141), channel_id=1, replica_groups=mesh['parts'=1,'data'=32] {'data'}, use_global_device_ids=true, to_apply=%region_2.2 | all-reduce | flops 7040 | bytes 56320 | tf_op jit(solution)/shard_map/while/body/eval_jaxpr/psum | solution.py:20
  2128.6 44.8 %all-reduce.2 = (f32[54,128]{1,0:T(8,128)S(1)}, f32[128]{0:T(128)S(1)}) all-reduce(f32[54,128]{1,0:T(8,128)S(1)} %convolution_bitcast_fusion.3, f32[128]{0:T(128)S(1)} %get-tuple-element.141), channel_id=1, replica_groups=mesh['parts'=1,'data'=32] {'data'}, use_global_device_ids=true, to_apply=%region_2.2 | all-reduce | flops 7040 | bytes 56320 | tf_op jit(solution)/shard_map/while/body/eval_jaxpr/psum | solution.py:20
  2177.9 44.8 %all-reduce.2 = (f32[54,128]{1,0:T(8,128)S(1)}, f32[128]{0:T(128)S(1)}) all-reduce(f32[54,128]{1,0:T(8,128)S(1)} %convolution_bitcast_fusion.3, f32[128]{0:T(128)S(1)} %get-tuple-element.141), channel_id=1, replica_groups=mesh['parts'=1,'data'=32] {'data'}, use_global_device_ids=true, to_apply=%region_2.2 | all-reduce | flops 7040 | bytes 56320 | tf_op jit(solution)/shard_map/while/body/eval_jaxpr/psum | solution.py:20
  2227.3 44.8 %all-reduce.2 = (f32[54,128]{1,0:T(8,128)S(1)}, f32[128]{0:T(128)S(1)}) all-reduce(f32[54,128]{1,0:T(8,128)S(1)} %convolution_bitcast_fusion.3, f32[128]{0:T(128)S(1)} %get-tuple-element.141), channel_id=1, replica_groups=mesh['parts'=1,'data'=32] {'data'}, use_global_device_ids=true, to_apply=%region_2.2 | all-reduce | flops 7040 | bytes 56320 | tf_op jit(solution)/shard_map/while/body/eval_jaxpr/psum | solution.py:20
  2276.6 44.8 %all-reduce.2 = (f32[54,128]{1,0:T(8,128)S(1)}, f32[128]{0:T(128)S(1)}) all-reduce(f32[54,128]{1,0:T(8,128)S(1)} %convolution_bitcast_fusion.3, f32[128]{0:T(128)S(1)} %get-tuple-element.141), channel_id=1, replica_groups=mesh['parts'=1,'data'=32] {'data'}, use_global_device_ids=true, to_apply=%region_2.2 | all-reduce | flops 7040 | bytes 56320 | tf_op jit(solution)/shard_map/while/body/eval_jaxpr/psum | solution.py:20
  2325.9 44.8 %all-reduce.2 = (f32[54,128]{1,0:T(8,128)S(1)}, f32[128]{0:T(128)S(1)}) all-reduce(f32[54,128]{1,0:T(8,128)S(1)} %convolution_bitcast_fusion.3, f32[128]{0:T(128)S(1)} %get-tuple-element.141), channel_id=1, replica_groups=mesh['parts'=1,'data'=32] {'data'}, use_global_device_ids=true, to_apply=%region_2.2 | all-reduce | flops 7040 | bytes 56320 | tf_op jit(solution)/shard_map/while/body/eval_jaxpr/psum | solution.py:20
  2375.3 44.8 %all-reduce.2 = (f32[54,128]{1,0:T(8,128)S(1)}, f32[128]{0:T(128)S(1)}) all-reduce(f32[54,128]{1,0:T(8,128)S(1)} %convolution_bitcast_fusion.3, f32[128]{0:T(128)S(1)} %get-tuple-element.141), channel_id=1, replica_groups=mesh['parts'=1,'data'=32] {'data'}, use_global_device_ids=true, to_apply=%region_2.2 | all-reduce | flops 7040 | bytes 56320 | tf_op jit(solution)/shard_map/while/body/eval_jaxpr/psum | solution.py:20
  2424.6 44.8 %all-reduce.2 = (f32[54,128]{1,0:T(8,128)S(1)}, f32[128]{0:T(128)S(1)}) all-reduce(f32[54,128]{1,0:T(8,128)S(1)} %convolution_bitcast_fusion.3, f32[128]{0:T(128)S(1)} %get-tuple-element.141), channel_id=1, replica_groups=mesh['parts'=1,'data'=32] {'data'}, use_global_device_ids=true, to_apply=%region_2.2 | all-reduce | flops 7040 | bytes 56320 | tf_op jit(solution)/shard_map/while/body/eval_jaxpr/psum | solution.py:20
  2473.9 44.8 %all-reduce.2 = (f32[54,128]{1,0:T(8,128)S(1)}, f32[128]{0:T(128)S(1)}) all-reduce(f32[54,128]{1,0:T(8,128)S(1)} %convolution_bitcast_fusion.3, f32[128]{0:T(128)S(1)} %get-tuple-element.141), channel_id=1, replica_groups=mesh['parts'=1,'data'=32] {'data'}, use_global_device_ids=true, to_apply=%region_2.2 | all-reduce | flops 7040 | bytes 56320 | tf_op jit(solution)/shard_map/while/body/eval_jaxpr/psum | solution.py:20
  2523.2 44.8 %all-reduce.2 = (f32[54,128]{1,0:T(8,128)S(1)}, f32[128]{0:T(128)S(1)}) all-reduce(f32[54,128]{1,0:T(8,128)S(1)} %convolution_bitcast_fusion.3, f32[128]{0:T(128)S(1)} %get-tuple-element.141), channel_id=1, replica_groups=mesh['parts'=1,'data'=32] {'data'}, use_global_device_ids=true, to_apply=%region_2.2 | all-reduce | flops 7040 | bytes 56320 | tf_op jit(solution)/shard_map/while/body/eval_jaxpr/psum | solution.py:20
  2572.6 44.8 %all-reduce.2 = (f32[54,128]{1,0:T(8,128)S(1)}, f32[128]{0:T(128)S(1)}) all-reduce(f32[54,128]{1,0:T(8,128)S(1)} %convolution_bitcast_fusion.3, f32[128]{0:T(128)S(1)} %get-tuple-element.141), channel_id=1, replica_groups=mesh['parts'=1,'data'=32] {'data'}, use_global_device_ids=true, to_apply=%region_2.2 | all-reduce | flops 7040 | bytes 56320 | tf_op jit(solution)/shard_map/while/body/eval_jaxpr/psum | solution.py:20
  2621.9 44.8 %all-reduce.2 = (f32[54,128]{1,0:T(8,128)S(1)}, f32[128]{0:T(128)S(1)}) all-reduce(f32[54,128]{1,0:T(8,128)S(1)} %convolution_bitcast_fusion.3, f32[128]{0:T(128)S(1)} %get-tuple-element.141), channel_id=1, replica_groups=mesh['parts'=1,'data'=32] {'data'}, use_global_device_ids=true, to_apply=%region_2.2 | all-reduce | flops 7040 | bytes 56320 | tf_op jit(solution)/shard_map/while/body/eval_jaxpr/psum | solution.py:20
  2671.3 44.8 %all-reduce.2 = (f32[54,128]{1,0:T(8,128)S(1)}, f32[128]{0:T(128)S(1)}) all-reduce(f32[54,128]{1,0:T(8,128)S(1)} %convolution_bitcast_fusion.3, f32[128]{0:T(128)S(1)} %get-tuple-element.141), channel_id=1, replica_groups=mesh['parts'=1,'data'=32] {'data'}, use_global_device_ids=true, to_apply=%region_2.2 | all-reduce | flops 7040 | bytes 56320 | tf_op jit(solution)/shard_map/while/body/eval_jaxpr/psum | solution.py:20
  2720.6 44.8 %all-reduce.2 = (f32[54,128]{1,0:T(8,128)S(1)}, f32[128]{0:T(128)S(1)}) all-reduce(f32[54,128]{1,0:T(8,128)S(1)} %convolution_bitcast_fusion.3, f32[128]{0:T(128)S(1)} %get-tuple-element.141), channel_id=1, replica_groups=mesh['parts'=1,'data'=32] {'data'}, use_global_device_ids=true, to_apply=%region_2.2 | all-reduce | flops 7040 | bytes 56320 | tf_op jit(solution)/shard_map/while/body/eval_jaxpr/psum | solution.py:20
  2769.9 44.8 %all-reduce.2 = (f32[54,128]{1,0:T(8,128)S(1)}, f32[128]{0:T(128)S(1)}) all-reduce(f32[54,128]{1,0:T(8,128)S(1)} %convolution_bitcast_fusion.3, f32[128]{0:T(128)S(1)} %get-tuple-element.141), channel_id=1, replica_groups=mesh['parts'=1,'data'=32] {'data'}, use_global_device_ids=true, to_apply=%region_2.2 | all-reduce | flops 7040 | bytes 56320 | tf_op jit(solution)/shard_map/while/body/eval_jaxpr/psum | solution.py:20
  2819.3 44.8 %all-reduce.2 = (f32[54,128]{1,0:T(8,128)S(1)}, f32[128]{0:T(128)S(1)}) all-reduce(f32[54,128]{1,0:T(8,128)S(1)} %convolution_bitcast_fusion.3, f32[128]{0:T(128)S(1)} %get-tuple-element.141), channel_id=1, replica_groups=mesh['parts'=1,'data'=32] {'data'}, use_global_device_ids=true, to_apply=%region_2.2 | all-reduce | flops 7040 | bytes 56320 | tf_op jit(solution)/shard_map/while/body/eval_jaxpr/psum | solution.py:20
  2868.6 44.8 %all-reduce.2 = (f32[54,128]{1,0:T(8,128)S(1)}, f32[128]{0:T(128)S(1)}) all-reduce(f32[54,128]{1,0:T(8,128)S(1)} %convolution_bitcast_fusion.3, f32[128]{0:T(128)S(1)} %get-tuple-element.141), channel_id=1, replica_groups=mesh['parts'=1,'data'=32] {'data'}, use_global_device_ids=true, to_apply=%region_2.2 | all-reduce | flops 7040 | bytes 56320 | tf_op jit(solution)/shard_map/while/body/eval_jaxpr/psum | solution.py:20
  2917.9 44.8 %all-reduce.2 = (f32[54,128]{1,0:T(8,128)S(1)}, f32[128]{0:T(128)S(1)}) all-reduce(f32[54,128]{1,0:T(8,128)S(1)} %convolution_bitcast_fusion.3, f32[128]{0:T(128)S(1)} %get-tuple-element.141), channel_id=1, replica_groups=mesh['parts'=1,'data'=32] {'data'}, use_global_device_ids=true, to_apply=%region_2.2 | all-reduce | flops 7040 | bytes 56320 | tf_op jit(solution)/shard_map/while/body/eval_jaxpr/psum | solution.py:20
  2967.3 44.8 %all-reduce.2 = (f32[54,128]{1,0:T(8,128)S(1)}, f32[128]{0:T(128)S(1)}) all-reduce(f32[54,128]{1,0:T(8,128)S(1)} %convolution_bitcast_fusion.3, f32[128]{0:T(128)S(1)} %get-tuple-element.141), channel_id=1, replica_groups=mesh['parts'=1,'data'=32] {'data'}, use_global_device_ids=true, to_apply=%region_2.2 | all-reduce | flops 7040 | bytes 56320 | tf_op jit(solution)/shard_map/while/body/eval_jaxpr/psum | solution.py:20
  3016.6 44.8 %all-reduce.2 = (f32[54,128]{1,0:T(8,128)S(1)}, f32[128]{0:T(128)S(1)}) all-reduce(f32[54,128]{1,0:T(8,128)S(1)} %convolution_bitcast_fusion.3, f32[128]{0:T(128)S(1)} %get-tuple-element.141), channel_id=1, replica_groups=mesh['parts'=1,'data'=32] {'data'}, use_global_device_ids=true, to_apply=%region_2.2 | all-reduce | flops 7040 | bytes 56320 | tf_op jit(solution)/shard_map/while/body/eval_jaxpr/psum | solution.py:20
  3065.9 44.8 %all-reduce.2 = (f32[54,128]{1,0:T(8,128)S(1)}, f32[128]{0:T(128)S(1)}) all-reduce(f32[54,128]{1,0:T(8,128)S(1)} %convolution_bitcast_fusion.3, f32[128]{0:T(128)S(1)} %get-tuple-element.141), channel_id=1, replica_groups=mesh['parts'=1,'data'=32] {'data'}, use_global_device_ids=true, to_apply=%region_2.2 | all-reduce | flops 7040 | bytes 56320 | tf_op jit(solution)/shard_map/while/body/eval_jaxpr/psum | solution.py:20
  3115.3 44.8 %all-reduce.2 = (f32[54,128]{1,0:T(8,128)S(1)}, f32[128]{0:T(128)S(1)}) all-reduce(f32[54,128]{1,0:T(8,128)S(1)} %convolution_bitcast_fusion.3, f32[128]{0:T(128)S(1)} %get-tuple-element.141), channel_id=1, replica_groups=mesh['parts'=1,'data'=32] {'data'}, use_global_device_ids=true, to_apply=%region_2.2 | all-reduce | flops 7040 | bytes 56320 | tf_op jit(solution)/shard_map/while/body/eval_jaxpr/psum | solution.py:20
  3164.6 44.8 %all-reduce.2 = (f32[54,128]{1,0:T(8,128)S(1)}, f32[128]{0:T(128)S(1)}) all-reduce(f32[54,128]{1,0:T(8,128)S(1)} %convolution_bitcast_fusion.3, f32[128]{0:T(128)S(1)} %get-tuple-element.141), channel_id=1, replica_groups=mesh['parts'=1,'data'=32] {'data'}, use_global_device_ids=true, to_apply=%region_2.2 | all-reduce | flops 7040 | bytes 56320 | tf_op jit(solution)/shard_map/while/body/eval_jaxpr/psum | solution.py:20
  (463 shorter events, 380.5 us)
Async XLA Ops:
  2.1 52.4 %copy-start.2 = (f32[54,128]{1,0:T(8,128)S(1)}, f32[54,128]{1,0:T(8,128)}, u32[]{:S(2)}) copy-start(f32[54,128]{1,0:T(8,128)} %param.10) | copy-start | bytes 82948
  2.1 52.4 %copy-start.3 = (bf16[4096,54]{0,1:T(8,128)(2,1)S(1)}, bf16[4096,54]{0,1:T(8,128)(2,1)}, u32[]{:S(2)}) copy-start(bf16[4096,54]{0,1:T(8,128)(2,1)} %param.7) | copy-start | bytes 1327108
  3210.8 0.6 copy-start
  3210.8 0.6 copy-start.1
where the time goes:
time: 3230 us; the launch traced here: 3210 us
  blocking collectives  2920 us (90%)
  matrix products  158 us (5%)
  local copies, waits for them, and re-layouts  84.4 us (3%)
  other arithmetic  49.8 us (2%)
    psum x65, blocking collectives, gradient_at(): gradient = lax.psum(grad_part, 'data') - positions / PRIOR_VAR  2920 us
    dot_general x64, matrix products, gradient_at(): jnp.dot(feat_rows, positions.astype(jnp.bfloat16), preferred_element_type...  104 us
    dynamic_update_slice x64, local copies, waits for them, and re-layouts, local_chains(): lax.scan(leap_step, (pos_init, mom_init, grad_init), step_sizes)  83 us

commit v1 on v0

v1 whole, which is shorter than its diff:
```python
import functools

import jax
import jax.numpy as jnp
from jax import lax
from jax.experimental import pallas as pl
from jax.experimental.pallas import tpu as pltpu
from jax.sharding import PartitionSpec as P

PRIOR_VAR = 4.0
MESH = pl.DeviceIdType.MESH
SHARERS = 2
LANES = 128
FPAD = 64
BLOCKS = 4


def chain_kernel(
    n_dev, xt_ref, x_ref, pos_ref, mom_ref, step_ref, pos_out, mom_out, energy_out,
    eps_buf, part_buf, mine_buf, gath_buf, send_sem, recv_sem, fin_send, fin_recv, hsend, hrecv, hmine, hpart,
):
    feats, chains_all = pos_ref.shape
    steps = step_ref.shape[0]
    groups = n_dev // SHARERS
    chains = chains_all // groups
    n_chunk = xt_ref.shape[0]
    me = lax.axis_index("data")
    share = lax.rem(me, SHARERS)
    group = me // SHARERS
    lane = lax.broadcasted_iota(jnp.int32, (chains, LANES), 1)
    low = lane < FPAD

    barrier = pltpu.get_barrier_semaphore()
    for off in range(1, n_dev):
        pl.semaphore_signal(barrier, inc=1, device_id={"data": lax.rem(me + off, n_dev)}, device_id_type=MESH)
    pl.semaphore_wait(barrier, n_dev - 1)

    def own_rows(ref):
        rows = ref.shape[0]
        padded = jnp.concatenate([ref[...], jnp.zeros((LANES - rows, chains_all), jnp.float32)], axis=0)
        return padded.T

    def doubled(ref, buf):
        wide = own_rows(ref)
        wide = jnp.where(lax.broadcasted_iota(jnp.int32, wide.shape, 1) < FPAD, wide, 0.0)
        buf[...] = wide + pltpu.roll(wide, FPAD, 1)
        return buf[pl.ds(pl.multiple_of(group * chains, chains), chains), :]

    theta0 = doubled(pos_ref, gath_buf.at[0])
    mom0 = doubled(mom_ref, gath_buf.at[0])
    eps_rows = doubled(step_ref, gath_buf.at[0])
    for l in range(steps):
        eps_buf[l + 1] = jnp.broadcast_to(eps_rows[:, l : l + 1], (chains, LANES))
    eps_buf[0] = jnp.zeros((chains, LANES), jnp.float32)

    def step_body(l, state):
        theta, mom, grad, carried, hmat = state
        eps = eps_buf[l]
        start_mom = mom
        mom = mom + 0.5 * eps * grad
        theta = theta + eps * mom

        half = 0.5 * theta
        left, right, none = jnp.where(low, half, 0.0), jnp.where(low, 0.0, half), jnp.zeros_like(half)
        weights = jnp.concatenate(
            [
                jnp.concatenate([left, none], axis=1),
                jnp.concatenate([right, none], axis=1),
                jnp.concatenate([none, left], axis=1),
                jnp.concatenate([none, right], axis=1),
            ],
            axis=0,
        ).astype(jnp.bfloat16)

        total = jnp.zeros((BLOCKS * chains, BLOCKS * FPAD), jnp.float32)
        ramp = jnp.zeros((BLOCKS * chains, 256), jnp.float32)
        prod = jnp.ones((BLOCKS * chains, 256), jnp.float32)
        for k in range(n_chunk):
            u = jnp.dot(weights, xt_ref[k], preferred_element_type=jnp.float32)
            h = jnp.tanh(u)
            resid = (1.0 + h).astype(jnp.bfloat16)
            total = total + jnp.dot(resid, x_ref[k], preferred_element_type=jnp.float32)
            pos_part = jnp.maximum(u, 0.0)
            fac = 1.0 + jnp.abs(h)
            for q in range(u.shape[1] // 256):
                ramp = ramp + pos_part[:, q * 256 : (q + 1) * 256]
                prod = prod * fac[:, q * 256 : (q + 1) * 256]

        blocks = [total[b * chains : (b + 1) * chains] for b in range(BLOCKS)]
        diag = jnp.where(low, blocks[0][:, :LANES] + blocks[2][:, LANES:], blocks[1][:, :LANES] + blocks[3][:, LANES:])
        mine = diag + pltpu.roll(diag, FPAD, 1)
        slot = lax.rem(l, 2)
        mine_buf[slot] = mine
        part_buf[slot, share] = mine
        copies = []
        for off in range(1, SHARERS):
            peer = group * SHARERS + lax.rem(share + off, SHARERS)
            copies.append(
                pltpu.make_async_remote_copy(
                    src_ref=mine_buf.at[slot],
                    dst_ref=part_buf.at[slot, share],
                    send_sem=send_sem.at[slot, off - 1],
                    recv_sem=recv_sem.at[slot, off - 1],
                    device_id={"data": peer},
                    device_id_type=MESH,
                )
            )
        for copy in copies:
            copy.start()

        kinetic = jnp.where(low, start_mom * start_mom * (0.5 / SHARERS), 0.0)
        hmat = jnp.where(lane == l - 2, jnp.sum(carried + kinetic, axis=1, keepdims=True), hmat)
        factors = SHARERS * 4096
        loss = 2.0 * ramp - jnp.log(prod)
        loss = loss[:, :LANES] + loss[:, LANES:]
        loss = loss[:chains] + loss[chains : 2 * chains] + loss[2 * chains : 3 * chains] + loss[3 * chains :]
        rows_per_lane = n_chunk * xt_ref.shape[2] * BLOCKS // LANES
        loss = loss + rows_per_lane * 0.6931471805599453
        carried = loss + jnp.where(low, theta * theta * (0.5 / PRIOR_VAR / SHARERS), 0.0)

        for copy in copies:
            copy.wait()
        summed = part_buf[slot, 0]
        for s in range(1, SHARERS):
            summed = summed + part_buf[slot, s]
        grad = -0.5 * summed - theta / PRIOR_VAR
        mom = mom + 0.5 * eps * grad
        return theta, mom, grad, carried, hmat

    zero = jnp.zeros((chains, LANES), jnp.float32)
    theta, mom, _, carried, hmat = lax.fori_loop(0, steps + 1, step_body, (theta0, mom0, zero, zero, zero))
    kinetic = jnp.where(low, mom * mom * (0.5 / SHARERS), 0.0)
    hmat = jnp.where(lane == steps - 1, jnp.sum(carried + kinetic, axis=1, keepdims=True), hmat)

    hmine[...] = hmat
    hpart[share] = hmat
    copies = []
    for off in range(1, SHARERS):
        peer = group * SHARERS + lax.rem(share + off, SHARERS)
        copies.append(
            pltpu.make_async_remote_copy(
                src_ref=hmine,
                dst_ref=hpart.at[share],
                send_sem=hsend.at[off - 1],
                recv_sem=hrecv.at[off - 1],
                device_id={"data": peer},
                device_id_type=MESH,
            )
        )
    for copy in copies:
        copy.start()
    for copy in copies:
        copy.wait()
    hsum = hpart[0]
    for s in range(1, SHARERS):
        hsum = hsum + hpart[s]

    rows = pl.ds(pl.multiple_of(group * chains, chains), chains)
    gath_buf[1, rows, :] = jnp.where(low, theta, mom)
    gath_buf[2, rows, :] = hsum
    copies = []
    for off in range(1, groups):
        peer = lax.rem(group + off, groups) * SHARERS + share
        copies.append(
            pltpu.make_async_remote_copy(
                src_ref=gath_buf.at[pl.ds(1, 2), rows, :],
                dst_ref=gath_buf.at[pl.ds(1, 2), rows, :],
                send_sem=fin_send.at[off - 1],
                recv_sem=fin_recv.at[off - 1],
                device_id={"data": peer},
                device_id_type=MESH,
            )
        )
    for copy in copies:
        copy.start()
    for copy in copies:
        copy.wait()
    both = gath_buf[1].T
    pos_out[...] = both[:feats]
    mom_out[...] = both[FPAD : FPAD + feats]
    energy_out[...] = gath_buf[2].T[:steps]


def solution(mesh):
    n_dev = mesh.shape["data"]
    groups = n_dev // SHARERS
    row_spec = P("data", None)
    chain_spec = P(None, "parts")

    def local_chains(feat_rows, labels, pos_init, mom_init, step_sizes):
        rows, feats = feat_rows.shape
        chains_all = pos_init.shape[1]
        steps = step_sizes.shape[0]
        chains = chains_all // groups
        signed = feat_rows * (1 - 2 * labels).astype(jnp.bfloat16)[:, None]
        signed = jnp.pad(signed, ((0, 0), (0, FPAD - feats)))
        packed = signed.reshape(BLOCKS, rows // BLOCKS, FPAD).transpose(1, 0, 2).reshape(rows // BLOCKS, BLOCKS * FPAD)
        same_share = [[g * SHARERS + s for g in range(groups)] for s in range(SHARERS)]
        x_all = lax.all_gather(packed, "data", axis_index_groups=same_share)
        xt_all = x_all.transpose(0, 2, 1)

        vmem = pl.BlockSpec(memory_space=pltpu.VMEM)
        dma = pltpu.SemaphoreType.DMA
        return pl.pallas_call(
            functools.partial(chain_kernel, n_dev),
            out_shape=(
                jax.ShapeDtypeStruct(pos_init.shape, jnp.float32),
                jax.ShapeDtypeStruct(mom_init.shape, jnp.float32),
                jax.ShapeDtypeStruct(step_sizes.shape, jnp.float32),
            ),
            in_specs=[vmem] * 5,
            out_specs=(vmem, vmem, vmem),
            scratch_shapes=[
                pltpu.VMEM((steps + 1, chains, LANES), jnp.float32),
                pltpu.VMEM((2, SHARERS, chains, LANES), jnp.float32),
                pltpu.VMEM((2, chains, LANES), jnp.float32),
                pltpu.VMEM((3, chains_all, LANES), jnp.float32),
                dma((2, SHARERS - 1)),
                dma((2, SHARERS - 1)),
                dma((groups - 1,)),
                dma((groups - 1,)),
                dma((SHARERS - 1,)),
                dma((SHARERS - 1,)),
                pltpu.VMEM((chains, LANES), jnp.float32),
                pltpu.VMEM((SHARERS, chains, LANES), jnp.float32),
            ],
            compiler_params=pltpu.CompilerParams(
                collective_id=0, has_side_effects=True, vmem_limit_bytes=60 * 1024 * 1024
            ),
        )(xt_all, x_all, pos_init, mom_init, step_sizes)

    return jax.shard_map(local_chains, mesh=mesh, in_specs=(row_spec, P("data"), chain_spec, chain_spec, chain_spec), out_specs=(chain_spec, chain_spec, chain_spec), check_vma=False)
```

time: 3230 us -> 352 us (0.11)
  blocking collectives: 2920 us -> 0 us
  Pallas kernels: 0 us -> 248 us
  matrix products: 158 us -> 0 us
  waiting for transfers between devices: 0 us -> 69.3 us
  local copies, waits for them, and re-layouts: 84.4 us -> 18 us
  other arithmetic: 49.8 us -> 1.78 us
    psum x65 -> x0, blocking collectives: 2920 us -> none  [gradient_at(): gradient = lax.psum(grad_part, 'data') - positions / PRIOR_VAR]
    pallas_call x0 -> x1, Pallas kernels: none -> 248 us  [local_chains(): pl.pallas_call(functools.partial(chain_kernel, n_dev), out_shape=(jax.Sha...]
    dot_general x129 -> x0, matrix products: 158 us -> none  [the longest x64 104 us: gradient_at(): jnp.dot(feat_rows, positions.astype(jnp.bfloat16), preferred_element_type...]
    dynamic_update_slice x64 -> x0, local copies, waits for them, and re-layouts: 83 us -> none  [local_chains(): lax.scan(leap_step, (pos_init, mom_init, grad_init), step_sizes)]
    all_gather x0 -> x1, waiting for transfers between devices: none -> 69.3 us  [local_chains(): x_all = lax.all_gather(packed, 'data', axis_index_groups=same_share)]
    mul x64 -> x1, other arithmetic: 44.3 us -> 1.05 us  [local_chains(): signed = feat_rows * (1 - 2 * labels).astype(jnp.bfloat16)[:, None]]
  transfers between devices with their start and end apart: 0 -> 1, of which waited for: 0 -> 1; matrix products, arithmetic and copies ran while one was open for 0% -> 0% of each run, Pallas kernels for 0% -> 0%
where the time goes in v1:
time: 352 us; the launch traced here: 351 us
  Pallas kernels  248 us (70%)
  waiting for transfers between devices  69.3 us (20%)
  local copies, waits for them, and re-layouts  18 us (5%)
  between operations  14.1 us (4%)
    pallas_call x1, Pallas kernels, local_chains(): pl.pallas_call(functools.partial(chain_kernel, n_dev), out_shape=(jax.Sha...  248 us
    all_gather x1, waiting for transfers between devices, local_chains(): x_all = lax.all_gather(packed, 'data', axis_index_groups=same_share)  69.3 us
    all_gather x1, local copies, waits for them, and re-layouts, local_chains(): x_all = lax.all_gather(packed, 'data', axis_index_groups=same_share)  12.3 us
  transfers between devices with their start and end apart: 1, of which 1 were waited for; matrix products, arithmetic and copies ran while one was open for 0% of the time, Pallas kernels for 0%

profile of v1, /device:TPU:97, one launch (start us, length us, event | category | flops | bytes accessed | tf_op | source)
XLA Modules:
  0.0 351.0 jit_solution(8591943899473641985)
XLA Ops:
  7.2 0.1 all-gather.2.cloned.1.call-start
  7.2 0.7 subtract_convert_fusion
  8.0 1.1 broadcast_multiply_fusion
  9.1 0.4 reshape.10
  9.5 0.2 copy.15
  9.6 1.0 copy.16
  10.7 0.1 all-gather.2.cloned.1.call-update
  10.7 69.3 %all-gather.2.cloned.1.call-done.x_ref = bf16[16,1024,256]{2,1,0:T(8,128)(2,1)} async-done(((bf16[1,1024,256]{2,1,0:T(8,128)(2,1)}), bf16[16,1024,256]{2,1,0:T(8,128)(2,1)}) %all-gather.2.cloned.1.call-update) | async-done | bytes 8388624 | tf_op jit(solution)/shard_map/all_gather | solution.py:199
  80.0 12.3 %copy.17 = bf16[16,1024,256]{1,2,0:T(8,128)(2,1)} copy(bf16[16,1024,256]{2,1,0:T(8,128)(2,1)} %all-gather.2.cloned.1.call-done.x_ref) | data formatting | bytes 16777216 | tf_op jit(solution)/shard_map/all_gather | solution.py:199
  92.3 247.8 %shard_map.76 = (f32[54,128]{1,0:T(8,128)}, f32[54,128]{1,0:T(8,128)}, f32[64,128]{1,0:T(8,128)}) custom-call(bf16[16,256,1024]{2,1,0:T(8,128)(2,1)} %bitcast.5, bf16[16,1024,256]{2,1,0:T(8,128)(2,1)} %all-gather.2.cloned.1.call-done.x_ref, f32[54,128]{1,0:T(8,128)} %pos_ref.1, f32[54,128]{1,0:T(8,128)} %mom_ref.1, f32[64,128]{1,0:T(8,128)} %step_ref.1), custom_call_target="tpu_custom_call" | custom-call | tf_op jit(solution)/shard_map/pallas_call | solution.py:204
  340.0 1.4 copy.21
  341.4 1.4 copy.22
  342.8 1.4 copy.23
  (1 shorter events, 0.0 us)
Async XLA Ops:
  7.2 72.8 %all-gather.2.cloned.1.call-start = ((), (), s32[]{:S(2)}) async-start(), calls=%async_computation | async-start | bytes 8912896 | tf_op jit(solution)/shard_map/all_gather | solution.py:199
Sparse Core Ops, SparseCore 0:
  10.8 69.1 all-gather.1

commit v2 on v1

v2 whole, which is shorter than its diff:
```python
import functools
import math

import jax
import jax.numpy as jnp
from jax import lax
from jax.experimental import pallas as pl
from jax.experimental.pallas import tpu as pltpu
from jax.sharding import PartitionSpec as P

PRIOR_VAR = 4.0
MESH = pl.DeviceIdType.MESH
CORES = 2
LANES = 128
FPAD = 64
BLOCKS = 4
TILE = 256
MID_LAG, GRAD_LAG, SWAP_LAG = 3, 4, 4
LN2 = 0.6931471805599453
OFFSETS = [(dx, dy) for dy in (0, -1, 1, 2) for dx in (0, -1, 1, 2)]
SHARED = [(0, 0), (-1, 0), (1, 0)]
ALONE = [o for o in OFFSETS if o not in SHARED]


def chain_kernel(
    n_dev, own_ref, pos_ref, mom_ref, step_ref, pos_out, mom_out, energy_out,
    xs, xt, eps_buf, part_buf, mine_buf, gath_buf,
    send_sem, recv_sem, fin_send, fin_recv, g_send, g_recv, d_send, d_recv, own_sem,
):
    feats, chains_all = pos_ref.shape
    steps = step_ref.shape[0]
    n_chip = n_dev // CORES
    side = math.isqrt(n_chip)
    chains = chains_all // n_chip
    pack_rows = own_ref.shape[0]
    half_rows, quarter = pack_rows // 2, pack_rows // 4
    n_slots = len(ALONE) + CORES * len(SHARED)
    me = lax.axis_index("data")
    core = lax.rem(me, CORES)
    chip = me // CORES
    chip_x, chip_y = lax.rem(chip, side), chip // side
    lane = lax.broadcasted_iota(jnp.int32, (chains, LANES), 1)
    low = lane < FPAD
    partner = {"data": chip * CORES + 1 - core}

    def neighbour(axis, step):
        nx = lax.rem(chip_x + side + step, side) if axis == 0 else chip_x
        ny = lax.rem(chip_y + side + step, side) if axis == 1 else chip_y
        return {"data": (ny * side + nx) * CORES + core}

    barrier = pltpu.get_barrier_semaphore()
    for off in range(1, n_dev):
        pl.semaphore_signal(barrier, inc=1, device_id={"data": lax.rem(me + off, n_dev)}, device_id_type=MESH)
    pl.semaphore_wait(barrier, n_dev - 1)

    def slot_of(offset):
        if offset in SHARED:
            return len(ALONE) + SHARED.index(offset) * CORES + core
        return ALONE.index(offset)

    sends = []

    def send(src, dst_slot, rows, sem, axis, step):
        copy = pltpu.make_async_remote_copy(
            src_ref=src,
            dst_ref=xs.at[dst_slot, rows, :],
            send_sem=g_send.at[len(sends)],
            recv_sem=g_recv.at[sem],
            device_id=neighbour(axis, step),
            device_id_type=MESH,
        )
        copy.start()
        sends.append(copy)

    def offset_of(half, first, second):
        return (first, second) if half == 0 else (second, first)

    def rows_of(half, part):
        if part is None:
            return pl.ds(half * half_rows, half_rows)
        return pl.ds(half * half_rows + part * quarter, quarter)

    kinds = [(1, None), (-1, None), (2, 0), (2, 1)]
    sem_ids = {}
    for half in range(2):
        for kind in kinds:
            sem_ids[half, kind[0], 0, kind[1]] = len(sem_ids)
            for first in (0, -1, 1, 2):
                sem_ids[half, first, kind[0], kind[1]] = len(sem_ids)

    def piece(half, first, second, part):
        return xs.at[slot_of(offset_of(half, first, second)), rows_of(half, part), :]

    def wrap(v):
        return 2 if v == -2 else v

    def pass_on(half, first, second, part, along, step, to_part=None):
        axis = along if half == 0 else 1 - along
        src_part = part if to_part is None else to_part
        if (first, second) == (0, 0):
            src = own_ref.at[rows_of(half, src_part), :]
        else:
            src = piece(half, first, second, src_part)
        nf, ns = (wrap(first - step), second) if along == 0 else (first, wrap(second - step))
        key = (half, nf, ns, to_part)
        send(src, slot_of(offset_of(half, nf, ns)), rows_of(half, src_part), sem_ids[key], axis, step)

    def arrive(half, first, second, part):
        dst = piece(half, first, second, part)
        pltpu.make_async_copy(dst, dst, g_recv.at[sem_ids[half, first, second, part]]).wait()

    handed = []

    def hand_over(half, offset, src):
        index = SHARED.index(offset) * 2 + half
        copy = pltpu.make_async_remote_copy(
            src_ref=src,
            dst_ref=xs.at[slot_of(offset), rows_of(half, None), :],
            send_sem=d_send.at[index],
            recv_sem=d_recv.at[index],
            device_id=partner,
            device_id_type=MESH,
        )
        copy.start()
        handed.append(copy)

    def turn(slot, half):
        def turn_part(i, _):
            rows = pl.ds(pl.multiple_of(half * half_rows + i * quarter, quarter), quarter)
            xt[slot, :, rows] = xs[slot, rows, :].T
            return 0

        lax.fori_loop(0, 2, turn_part, 0)

    for half in range(2):
        for step in (1, -1):
            pass_on(half, 0, 0, None, 0, step)
    for half in range(2):
        for step in (1, -1):
            pass_on(half, 0, 0, None, 1, step)
    own_slot = slot_of((0, 0))
    own_copy = pltpu.make_async_copy(own_ref, xs.at[own_slot], own_sem.at[0])
    own_copy.start()
    for half in range(2):
        hand_over(half, (0, 0), own_ref.at[rows_of(half, None), :])

    def own_rows(ref):
        rows = ref.shape[0]
        padded = jnp.concatenate([ref[...], jnp.zeros((LANES - rows, chains_all), jnp.float32)], axis=0)
        return padded.T

    def doubled(ref, buf):
        wide = own_rows(ref)
        buf[...] = wide + pltpu.roll(wide, FPAD, 1)
        return buf[pl.ds(pl.multiple_of(chip * chains, chains), chains), :]

    theta0 = doubled(pos_ref, gath_buf.at[0])
    mom0 = doubled(mom_ref, gath_buf.at[0])
    eps_rows = doubled(step_ref, gath_buf.at[0])
    for l in range(steps):
        eps_buf[l + 1] = jnp.broadcast_to(eps_rows[:, l : l + 1], (chains, LANES))
    eps_buf[0] = jnp.zeros((chains, LANES), jnp.float32)
    own_copy.wait()
    for half in range(2):
        turn(own_slot, half)

    def landed(half, first, second):
        offset = offset_of(half, first, second)
        if offset in SHARED:
            hand_over(half, offset, piece(half, first, second, None))

    fresh = []
    for half in range(2):
        for first in (-1, 1):
            arrive(half, first, 0, None)
            pass_on(half, first, 0, None, 0, -first, to_part=0 if first < 0 else 1)
            for step in (1, -1):
                pass_on(half, first, 0, None, 1, step)
            landed(half, first, 0)
            fresh.append((half, first, 0))

    def turn_fresh():
        for half, first, second in fresh:
            turn(slot_of(offset_of(half, first, second)), half)
        fresh.clear()

    turn_fresh()

    def second_ring(first):
        for half in range(2):
            for second in (-1, 1):
                arrive(half, first, second, None)
                pass_on(half, first, second, None, 1, -second, to_part=0 if second < 0 else 1)
                landed(half, first, second)
                fresh.append((half, first, second))

    second_ring(0)
    for half in range(2):
        for part in range(2):
            arrive(half, 2, 0, part)
        for step in (1, -1):
            pass_on(half, 2, 0, None, 1, step)
        fresh.append((half, 2, 0))
    turn_fresh()
    second_ring(-1)
    second_ring(1)
    turn_fresh()
    second_ring(2)
    for copy in handed:
        copy.wait_recv()
    for i, offset in enumerate(SHARED):
        for half in range(2):
            turn(len(ALONE) + i * CORES + 1 - core, half)
    for first in (0, -1, 1):
        for half in range(2):
            for part in range(2):
                arrive(half, first, 2, part)
            fresh.append((half, first, 2))
    turn_fresh()
    for half in range(2):
        for part in range(2):
            arrive(half, 2, 2, part)
        fresh.append((half, 2, 2))
    turn_fresh()
    for copy in sends:
        copy.wait_send()
    for copy in handed:
        copy.wait_send()

    def step_body(l, state):
        theta, mom, grad, carried, hmat = state
        eps = eps_buf[l]
        start_mom = mom
        mom = mom + 0.5 * eps * grad
        theta = theta + eps * mom

        half = 0.5 * theta
        left, right, none = jnp.where(low, half, 0.0), jnp.where(low, 0.0, half), jnp.zeros_like(half)
        weights = jnp.concatenate(
            [
                jnp.concatenate([left, none], axis=1),
                jnp.concatenate([right, none], axis=1),
                jnp.concatenate([none, left], axis=1),
                jnp.concatenate([none, right], axis=1),
            ],
            axis=0,
        ).astype(jnp.bfloat16)

        def gather_blocks(total):
            blocks = [total[b * chains : (b + 1) * chains] for b in range(BLOCKS)]
            diag = jnp.where(low, blocks[0][:, :LANES] + blocks[2][:, LANES:], blocks[1][:, :LANES] + blocks[3][:, LANES:])
            return diag + pltpu.roll(diag, FPAD, 1)

        def fold(sums):
            loss = 2.0 * sums[0] - jnp.log(sums[1])
            return loss[:chains] + loss[chains : 2 * chains] + loss[2 * chains : 3 * chains] + loss[3 * chains :]

        no_sums = (jnp.zeros((BLOCKS * chains, LANES), jnp.float32), jnp.ones((BLOCKS * chains, LANES), jnp.float32))
        slot = lax.rem(l, 2)
        copy = pltpu.make_async_remote_copy(
            src_ref=mine_buf.at[slot],
            dst_ref=part_buf.at[slot],
            send_sem=send_sem.at[slot],
            recv_sem=recv_sem.at[slot],
            device_id=partner,
            device_id_type=MESH,
        )
        per_shard = pack_rows // TILE
        tiles = [(k, slice(c * TILE, (c + 1) * TILE)) for k in range(n_slots) for c in range(per_shard)]
        n_alone = len(ALONE) * per_shard
        sums = [no_sums, no_sums]
        totals = [jnp.zeros((BLOCKS * chains, BLOCKS * FPAD), jnp.float32)] * 2
        logits, resids = {}, {}
        mine = None
        for turn_no in range(len(tiles) + GRAD_LAG):
            if turn_no < len(tiles):
                k, cols = tiles[turn_no]
                logits[turn_no] = jnp.dot(weights, xt[k, :, cols], preferred_element_type=jnp.float32)
            tile = turn_no - MID_LAG
            if 0 <= tile < len(tiles):
                u = logits.pop(tile)
                h = jnp.tanh(u)
                pos_part = jnp.maximum(u, 0.0)
                fac = 1.0 + jnp.abs(h)
                ramp, prod = sums[tile >= n_alone]
                for q in range(TILE // 256):
                    lo, hi = slice(q * 256, q * 256 + LANES), slice(q * 256 + LANES, (q + 1) * 256)
                    ramp = ramp + (pos_part[:, lo] + pos_part[:, hi])
                    prod = prod * (fac[:, lo] * fac[:, hi])
                sums[tile >= n_alone] = (ramp, prod)
                resids[tile] = (1.0 + h).astype(jnp.bfloat16)
            tile = turn_no - GRAD_LAG
            if tile >= 0:
                k, rows = tiles[tile]
                part = jnp.dot(resids.pop(tile), xs[k, rows, :], preferred_element_type=jnp.float32)
                totals[tile >= n_alone] = totals[tile >= n_alone] + part
            if tile == n_alone - 1 + SWAP_LAG:
                mine = gather_blocks(totals[0])
                mine_buf[slot] = mine
                copy.start()
        both = gather_blocks(totals[1])
        sums_alone, sums_both = sums

        kinetic = jnp.where(low, start_mom * start_mom * (0.5 / CORES), 0.0)
        hmat = jnp.where(lane == l - 2, jnp.sum(carried + kinetic, axis=1, keepdims=True), hmat)
        loss = fold(sums_alone) + (1.0 / CORES) * fold(sums_both)
        loss = loss + (n_chip * pack_rows * BLOCKS // LANES) * LN2
        carried = loss + jnp.where(low, theta * theta * (0.5 / PRIOR_VAR / CORES), 0.0)

        copy.wait()
        grad = -0.5 * ((mine + part_buf[slot]) + both) - theta / PRIOR_VAR
        mom = mom + 0.5 * eps * grad
        return theta, mom, grad, carried, hmat

    zero = jnp.zeros((chains, LANES), jnp.float32)
    theta, mom, _, carried, hmat = lax.fori_loop(0, steps + 1, step_body, (theta0, mom0, zero, zero, zero))
    kinetic = jnp.where(low, mom * mom * (0.5 / CORES), 0.0)
    hmat = jnp.where(lane == steps - 1, jnp.sum(carried + kinetic, axis=1, keepdims=True), hmat)

    last = (steps + 1) % 2
    mine_buf[last] = hmat
    copy = pltpu.make_async_remote_copy(
        src_ref=mine_buf.at[last],
        dst_ref=part_buf.at[last],
        send_sem=send_sem.at[last],
        recv_sem=recv_sem.at[last],
        device_id=partner,
        device_id_type=MESH,
    )
    copy.start()
    copy.wait()

    rows = pl.ds(pl.multiple_of(chip * chains, chains), chains)
    gath_buf[1, rows, :] = jnp.where(low, theta, mom)
    gath_buf[2, rows, :] = hmat + part_buf[last]
    copies = []
    for off in range(1, n_chip):
        copies.append(
            pltpu.make_async_remote_copy(
                src_ref=gath_buf.at[pl.ds(1, 2), rows, :],
                dst_ref=gath_buf.at[pl.ds(1, 2), rows, :],
                send_sem=fin_send.at[off - 1],
                recv_sem=fin_recv.at[off - 1],
                device_id={"data": lax.rem(chip + off, n_chip) * CORES + core},
                device_id_type=MESH,
            )
        )
    for copy in copies:
        copy.start()
    for copy in copies:
        copy.wait()
    ends = gath_buf[1].T
    pos_out[...] = ends[:feats]
    mom_out[...] = ends[FPAD : FPAD + feats]
    energy_out[...] = gath_buf[2].T[:steps]


def solution(mesh):
    n_dev = mesh.shape["data"]
    n_chip = n_dev // CORES
    row_spec = P("data", None)
    chain_spec = P(None, "parts")

    def local_chains(feat_rows, labels, pos_init, mom_init, step_sizes):
        rows, feats = feat_rows.shape
        chains_all = pos_init.shape[1]
        steps = step_sizes.shape[0]
        chains = chains_all // n_chip
        pack_rows, pack_cols = rows // BLOCKS, BLOCKS * FPAD
        signed = feat_rows * (1 - 2 * labels).astype(jnp.bfloat16)[:, None]
        signed = jnp.pad(signed, ((0, 0), (0, FPAD - feats)))
        packed = signed.reshape(BLOCKS, pack_rows, FPAD).transpose(1, 0, 2).reshape(pack_rows, pack_cols)

        vmem = pl.BlockSpec(memory_space=pltpu.VMEM)
        dma = pltpu.SemaphoreType.DMA
        slots = len(ALONE) + CORES * len(SHARED)
        return pl.pallas_call(
            functools.partial(chain_kernel, n_dev),
            out_shape=(
                jax.ShapeDtypeStruct(pos_init.shape, jnp.float32),
                jax.ShapeDtypeStruct(mom_init.shape, jnp.float32),
                jax.ShapeDtypeStruct(step_sizes.shape, jnp.float32),
            ),
            in_specs=[vmem] * 4,
            out_specs=(vmem, vmem, vmem),
            scratch_shapes=[
                pltpu.VMEM((slots, pack_rows, pack_cols), jnp.bfloat16),
                pltpu.VMEM((slots, pack_cols, pack_rows), jnp.bfloat16),
                pltpu.VMEM((steps + 1, chains, LANES), jnp.float32),
                pltpu.VMEM((2, chains, LANES), jnp.float32),
                pltpu.VMEM((2, chains, LANES), jnp.float32),
                pltpu.VMEM((3, chains_all, LANES), jnp.float32),
                dma((2,)),
                dma((2,)),
                dma((n_chip - 1,)),
                dma((n_chip - 1,)),
                dma((40,)),
                dma((40,)),
                dma((2 * len(SHARED),)),
                dma((2 * len(SHARED),)),
                dma((1,)),
            ],
            compiler_params=pltpu.CompilerParams(
                collective_id=0, has_side_effects=True, vmem_limit_bytes=60 * 1024 * 1024
            ),
        )(packed, pos_init, mom_init, step_sizes)

    return jax.shard_map(local_chains, mesh=mesh, in_specs=(row_spec, P("data"), chain_spec, chain_spec, chain_spec), out_specs=(chain_spec, chain_spec, chain_spec), check_vma=False)
```

time: 352 us -> 278 us (0.79)
  waiting for transfers between devices: 69.3 us -> 0 us
  Pallas kernels: 248 us -> 271 us
  local copies, waits for them, and re-layouts: 18 us -> 4.32 us
  between operations: 14.1 us -> 0.67 us
    all_gather x1 -> x0, waiting for transfers between devices: 69.3 us -> none  [local_chains(): x_all = lax.all_gather(packed, 'data', axis_index_groups=same_share)]
    pallas_call x1, Pallas kernels: 248 us -> 271 us  [local_chains(): pl.pallas_call(functools.partial(chain_kernel, n_dev), out_shape=(jax.Sha...]
    all_gather x1 -> x0, local copies, waits for them, and re-layouts: 12.3 us -> none  [local_chains(): x_all = lax.all_gather(packed, 'data', axis_index_groups=same_share)]
  transfers between devices with their start and end apart: 1 -> 0, of which waited for: 1 -> 0; matrix products, arithmetic and copies ran while one was open for 0% -> 0% of each run, Pallas kernels for 0% -> 0%
where the time goes in v2:
time: 278 us
  Pallas kernels  271 us (97%)
  local copies, waits for them, and re-layouts  4.32 us (2%)
    pallas_call x1, Pallas kernels, local_chains(): pl.pallas_call(functools.partial(chain_kernel, n_dev), out_shape=(jax.Sha...  271 us

profile of v2, /device:TPU:97, one launch (start us, length us, event | category | flops | bytes accessed | tf_op | source)
XLA Modules:
  0.0 278.1 jit_solution(8401356974557146798)
XLA Ops:
  0.6 0.7 subtract_convert_fusion
  1.4 1.1 broadcast_multiply_fusion
  2.5 0.4 reshape.13
  2.8 0.2 copy.10
  3.0 1.0 copy.11.own_ref
  4.0 271.3 %shard_map.76 = (f32[54,128]{1,0:T(8,128)}, f32[54,128]{1,0:T(8,128)}, f32[64,128]{1,0:T(8,128)}) custom-call(bf16[1024,256]{1,0:T(8,128)(2,1)} %copy.11.own_ref, f32[54,128]{1,0:T(8,128)} %pos_ref.1, f32[54,128]{1,0:T(8,128)} %mom_ref.1, f32[64,128]{1,0:T(8,128)} %step_ref.1), custom_call_target="tpu_custom_call" | custom-call | tf_op jit(solution)/shard_map/pallas_call | solution.py:377
  275.3 0.0 copy-start.1
  275.3 1.4 copy.15
  276.7 0.0 copy-done.1
  276.7 0.0 copy-start
  276.7 0.6 copy.16
  277.3 0.2 copy-done
  277.5 0.6 copy.17
  (1 shorter events, 0.0 us)
Async XLA Ops:
  275.3 1.4 copy-start.1
  276.7 0.8 copy-start

commit v3 on v2

v3 whole, which is shorter than its diff:
```python
import functools
import math

import jax
import jax.numpy as jnp
from jax import lax
from jax.experimental import pallas as pl
from jax.experimental.pallas import tpu as pltpu
from jax.sharding import PartitionSpec as P

PRIOR_VAR = 4.0
MESH = pl.DeviceIdType.MESH
CORES = 2
LANES = 128
FPAD = 56
BLOCKS = 16
UNIT = 8
MID_LAG, GRAD_LAG, SWAP_LAG = 2, 3, 2
LN2 = 0.6931471805599453
OFFSETS = [(dx, dy) for dy in (0, -1, 1, 2) for dx in (0, -1, 1, 2)]
SHARED = [(0, 0), (-1, 0), (1, 0)]
ALONE = [o for o in OFFSETS if o not in SHARED]


def chain_kernel(
    n_dev, rows_ref, label_ref, pos_ref, mom_ref, step_ref, all_out,
    xs, xt, eps_buf, part_buf, mine_buf, gath_buf,
    send_sem, recv_sem, fin_send, fin_recv, g_send, g_recv, d_send, d_recv,
):
    feats, chains_all = pos_ref.shape
    steps = step_ref.shape[0]
    n_chip = n_dev // CORES
    side = math.isqrt(n_chip)
    chains = chains_all // n_chip
    block_rows = xs.shape[1]
    width = BLOCKS * FPAD
    half_rows, quarter = width // 2, width // 4
    n_slots = len(ALONE) + CORES * len(SHARED)
    me = lax.axis_index("data")
    core = lax.rem(me, CORES)
    chip = me // CORES
    chip_x, chip_y = lax.rem(chip, side), chip // side
    lane = lax.broadcasted_iota(jnp.int32, (chains, LANES), 1)
    low = lane < feats
    partner = {"data": chip * CORES + 1 - core}

    def neighbour(axis, step):
        nx = lax.rem(chip_x + side + step, side) if axis == 0 else chip_x
        ny = lax.rem(chip_y + side + step, side) if axis == 1 else chip_y
        return {"data": (ny * side + nx) * CORES + core}

    barrier = pltpu.get_barrier_semaphore()
    for off in range(1, n_dev):
        pl.semaphore_signal(barrier, inc=1, device_id={"data": lax.rem(me + off, n_dev)}, device_id_type=MESH)

    def slot_of(offset):
        if offset in SHARED:
            return len(ALONE) + SHARED.index(offset) * CORES + core
        return ALONE.index(offset)

    sends = []

    def send(src, dst_slot, rows, sem, axis, step):
        copy = pltpu.make_async_remote_copy(
            src_ref=src,
            dst_ref=xt.at[dst_slot, rows, :],
            send_sem=g_send.at[len(sends)],
            recv_sem=g_recv.at[sem],
            device_id=neighbour(axis, step),
            device_id_type=MESH,
        )
        copy.start()
        sends.append(copy)

    def offset_of(half, first, second):
        return (first, second) if half == 0 else (second, first)

    def rows_of(half, part):
        if part is None:
            return pl.ds(half * half_rows, half_rows)
        return pl.ds(half * half_rows + part * quarter, quarter)

    kinds = [(1, None), (-1, None), (2, 0), (2, 1)]
    sem_ids = {}
    for half in range(2):
        for kind in kinds:
            sem_ids[half, kind[0], 0, kind[1]] = len(sem_ids)
            for first in (0, -1, 1, 2):
                sem_ids[half, first, kind[0], kind[1]] = len(sem_ids)

    def piece(half, first, second, part):
        return xt.at[slot_of(offset_of(half, first, second)), rows_of(half, part), :]

    def wrap(v):
        return 2 if v == -2 else v

    def pass_on(half, first, second, part, along, step, to_part=None):
        axis = along if half == 0 else 1 - along
        src_part = part if to_part is None else to_part
        src = piece(half, first, second, src_part)
        nf, ns = (wrap(first - step), second) if along == 0 else (first, wrap(second - step))
        key = (half, nf, ns, to_part)
        send(src, slot_of(offset_of(half, nf, ns)), rows_of(half, src_part), sem_ids[key], axis, step)

    def arrive(half, first, second, part):
        dst = piece(half, first, second, part)
        pltpu.make_async_copy(dst, dst, g_recv.at[sem_ids[half, first, second, part]]).wait()

    handed = []

    def hand_over(half, offset, src):
        index = SHARED.index(offset) * 2 + half
        copy = pltpu.make_async_remote_copy(
            src_ref=src,
            dst_ref=xt.at[slot_of(offset), rows_of(half, None), :],
            send_sem=d_send.at[index],
            recv_sem=d_recv.at[index],
            device_id=partner,
            device_id_type=MESH,
        )
        copy.start()
        handed.append(copy)

    seen = set()

    def turn(offset, half, slot):
        seen.add((offset, half))
        if (offset, 1 - half) not in seen:
            return

        def turn_part(i, _):
            rows = pl.ds(pl.multiple_of(i * LANES, LANES), LANES)
            xs[slot, :, rows] = xt[slot, rows, :].T
            return 0

        lax.fori_loop(0, width // LANES, turn_part, 0)

    own_slot = slot_of((0, 0))
    signs = (1 - 2 * label_ref[...]).astype(jnp.float32).astype(jnp.bfloat16)
    per_block = block_rows // LANES
    for j in range(BLOCKS * per_block):
        tile = rows_ref[:, j * LANES : (j + 1) * LANES] * signs[j : j + 1, :]
        tile = jnp.concatenate([tile, jnp.zeros((FPAD - feats, LANES), jnp.bfloat16)], axis=0)
        b, m = j // per_block, j % per_block
        xt[own_slot, b * FPAD : (b + 1) * FPAD, m * LANES : (m + 1) * LANES] = tile

    pl.semaphore_wait(barrier, n_dev - 1)
    for half in range(2):
        for step in (1, -1):
            pass_on(half, 0, 0, None, 0, step)
    for half in range(2):
        for step in (1, -1):
            pass_on(half, 0, 0, None, 1, step)
    for half in range(2):
        hand_over(half, (0, 0), piece(half, 0, 0, None))

    def own_rows(ref):
        rows = ref.shape[0]
        padded = jnp.concatenate([ref[...], jnp.zeros((LANES - rows, chains_all), jnp.float32)], axis=0)
        return padded.T

    def mine_of(ref, buf):
        buf[...] = own_rows(ref)
        return buf[pl.ds(pl.multiple_of(chip * chains, chains), chains), :]

    theta0 = mine_of(pos_ref, gath_buf.at[0])
    mom0 = mine_of(mom_ref, gath_buf.at[0])
    eps_rows = mine_of(step_ref, gath_buf.at[0])
    for l in range(steps):
        eps_buf[l + 1] = jnp.broadcast_to(eps_rows[:, l : l + 1], (chains, LANES))
    eps_buf[0] = jnp.zeros((chains, LANES), jnp.float32)
    for half in range(2):
        turn((0, 0), half, own_slot)

    def landed(half, first, second):
        offset = offset_of(half, first, second)
        if offset in SHARED:
            hand_over(half, offset, piece(half, first, second, None))

    fresh = []
    for half in range(2):
        for first in (-1, 1):
            arrive(half, first, 0, None)
            pass_on(half, first, 0, None, 0, -first, to_part=0 if first < 0 else 1)
            for step in (1, -1):
                pass_on(half, first, 0, None, 1, step)
            landed(half, first, 0)
            fresh.append((half, first, 0))

    def turn_fresh():
        for half, first, second in fresh:
            offset = offset_of(half, first, second)
            turn(offset, half, slot_of(offset))
        fresh.clear()

    turn_fresh()

    def second_ring(first):
        for half in range(2):
            for second in (-1, 1):
                arrive(half, first, second, None)
                pass_on(half, first, second, None, 1, -second, to_part=0 if second < 0 else 1)
                landed(half, first, second)
                fresh.append((half, first, second))

    second_ring(0)
    for half in range(2):
        for part in range(2):
            arrive(half, 2, 0, part)
        for step in (1, -1):
            pass_on(half, 2, 0, None, 1, step)
        fresh.append((half, 2, 0))
    turn_fresh()
    second_ring(-1)
    second_ring(1)
    turn_fresh()
    second_ring(2)
    for copy in handed:
        copy.wait_recv()
    for i, offset in enumerate(SHARED):
        for half in range(2):
            turn((offset, "partner"), half, len(ALONE) + i * CORES + 1 - core)
    for first in (0, -1, 1):
        for half in range(2):
            for part in range(2):
                arrive(half, first, 2, part)
            fresh.append((half, first, 2))
    turn_fresh()
    for half in range(2):
        for part in range(2):
            arrive(half, 2, 2, part)
        fresh.append((half, 2, 2))
    turn_fresh()
    for copy in sends:
        copy.wait_send()
    for copy in handed:
        copy.wait_send()

    def step_body(l, state):
        theta, mom, grad, carried, hmat = state
        eps = eps_buf[l]
        start_mom = mom
        mom = mom + 0.5 * eps * grad
        theta = theta + eps * mom

        half = 0.5 * theta
        none = jnp.zeros_like(half)
        rows_w = []
        for b in range(UNIT):
            col, start = b * FPAD // LANES, b * FPAD % LANES
            moved = pltpu.roll(half, start, 1) if start else half
            cols = [none] * (-(-UNIT * FPAD // LANES))
            if start + FPAD <= LANES:
                cols[col] = moved
            else:
                cols[col] = jnp.where(lane >= start, moved, 0.0)
                cols[col + 1] = jnp.where(lane >= start, 0.0, moved)
            rows_w.append(jnp.concatenate(cols, axis=1))
        weights = jnp.concatenate(rows_w, axis=0).astype(jnp.bfloat16)[:, : UNIT * FPAD]

        first_block = (0, 4, 8, 12)

        def gather_blocks(strips):
            result = None
            for b in range(BLOCKS):
                col, start = b * FPAD // LANES, b * FPAD % LANES

                def at(c):
                    strip = c // 2
                    row = (b - first_block[strip]) * chains
                    if strip < 3:
                        return strips[strip][row : row + chains, (c % 2) * LANES : (c % 2 + 1) * LANES]
                    other = row + 4 * chains
                    return strips[3][row : row + chains, :LANES] + strips[3][other : other + chains, LANES:]

                part = at(col)
                if start + feats > LANES:
                    part = jnp.where(lane >= start, part, at(col + 1))
                part = pltpu.roll(part, LANES - start, 1) if start else part
                result = part if result is None else result + part
            return jnp.where(low, result, 0.0)

        def fold(sums):
            loss = 2.0 * sums[0] - jnp.log(sums[1])
            return loss[:chains] + loss[chains : 2 * chains] + loss[2 * chains : 3 * chains] + loss[3 * chains :]

        no_sums = (jnp.zeros((4 * chains, LANES), jnp.float32), jnp.ones((4 * chains, LANES), jnp.float32))
        slot = lax.rem(l, 2)
        copy = pltpu.make_async_remote_copy(
            src_ref=mine_buf.at[slot],
            dst_ref=part_buf.at[slot],
            send_sem=send_sem.at[slot],
            recv_sem=recv_sem.at[slot],
            device_id=partner,
            device_id_type=MESH,
        )
        n_alone = len(ALONE)
        sums = [no_sums, no_sums]
        heights = (6 * chains, 6 * chains, 6 * chains, 8 * chains)
        totals = [[jnp.zeros((height, 256), jnp.float32) for height in heights] for _ in range(2)]
        resids = {}
        mine = None

        def logits_of(k, unit):
            return jnp.dot(weights, xt[k, unit * UNIT * FPAD : (unit + 1) * UNIT * FPAD, :], preferred_element_type=jnp.float32)

        def resids_of(u, which):
            h = jnp.tanh(u)
            pos_part = jnp.maximum(u, 0.0)
            fac = 1.0 + jnp.abs(h)
            pos_part = pos_part[: 4 * chains] + pos_part[4 * chains :]
            fac = fac[: 4 * chains] * fac[4 * chains :]
            ramp, prod = sums[which]
            sums[which] = (ramp + (pos_part[:, :LANES] + pos_part[:, LANES:]), prod * (fac[:, :LANES] * fac[:, LANES:]))
            return (1.0 + h).astype(jnp.bfloat16)

        def add_strip(which, strip, resid, cols):
            part = jnp.dot(resid, cols, preferred_element_type=jnp.float32)
            totals[which][strip] = totals[which][strip] + part

        def last_strips(which, ks):
            resid = jnp.concatenate([resids[k, 1][4 * chains :] for k in ks], axis=0)
            cols = jnp.concatenate([xs[k, :, 3 * 256 :] for k in ks], axis=1)
            if len(ks) == 1:
                part = jnp.dot(resid, cols, preferred_element_type=jnp.float32)
                zero_rows = jnp.zeros_like(part)
                part = jnp.concatenate([jnp.concatenate([part, zero_rows], axis=1), jnp.zeros((4 * chains, 256), jnp.float32)], axis=0)
                totals[which][3] = totals[which][3] + part
            else:
                add_strip(which, 3, resid, cols)

        def strips_of(k, stage):
            which = int(k >= n_alone)
            if stage == 0:
                add_strip(which, 0, resids[k, 0][: 6 * chains], xs[k, :, :256])
                mid = jnp.concatenate([resids[k, 0][4 * chains :], resids[k, 1][: 2 * chains]], axis=0)
                add_strip(which, 1, mid, xs[k, :, 256:512])
                return
            add_strip(which, 2, resids[k, 1][: 6 * chains], xs[k, :, 512:768])
            ends = k in (n_alone - 1, n_slots - 1)
            first = 0 if which == 0 else n_alone
            if (k - first) % 2:
                last_strips(which, [k - 1, k])
            elif ends:
                last_strips(which, [k])

        logits = {}
        units = 2 * n_slots
        for turn_no in range(units + GRAD_LAG):
            if turn_no < units:
                logits[turn_no] = logits_of(turn_no // 2, turn_no % 2)
            job = turn_no - MID_LAG
            if 0 <= job < units:
                resids[job // 2, job % 2] = resids_of(logits.pop(job), int(job // 2 >= n_alone))
            job = turn_no - GRAD_LAG
            if job >= 0:
                strips_of(job // 2, job % 2)
            if job == 2 * n_alone - 1 + SWAP_LAG:
                mine = gather_blocks(totals[0])
                mine_buf[slot] = mine
                copy.start()
        both = gather_blocks(totals[1])
        sums_alone, sums_both = sums

        kinetic = jnp.where(low, start_mom * start_mom * (0.5 / CORES), 0.0)
        hmat = jnp.where(lane == l - 2, jnp.sum(carried + kinetic, axis=1, keepdims=True), hmat)
        loss = fold(sums_alone) + (1.0 / CORES) * fold(sums_both)
        loss = loss + (n_chip * block_rows * BLOCKS // LANES) * LN2
        carried = loss + jnp.where(low, theta * theta * (0.5 / PRIOR_VAR / CORES), 0.0)

        copy.wait()
        grad = -0.5 * ((mine + part_buf[slot]) + both) - theta / PRIOR_VAR
        mom = mom + 0.5 * eps * grad
        return theta, mom, grad, carried, hmat

    zero = jnp.zeros((chains, LANES), jnp.float32)
    theta, mom, _, carried, hmat = lax.fori_loop(0, steps + 1, step_body, (theta0, mom0, zero, zero, zero))
    kinetic = jnp.where(low, mom * mom * (0.5 / CORES), 0.0)
    hmat = jnp.where(lane == steps - 1, jnp.sum(carried + kinetic, axis=1, keepdims=True), hmat)

    last = (steps + 1) % 2
    mine_buf[last] = hmat
    copy = pltpu.make_async_remote_copy(
        src_ref=mine_buf.at[last],
        dst_ref=part_buf.at[last],
        send_sem=send_sem.at[last],
        recv_sem=recv_sem.at[last],
        device_id=partner,
        device_id_type=MESH,
    )
    copy.start()
    copy.wait()

    rows = pl.ds(pl.multiple_of(chip * chains, chains), chains)
    gath_buf[1, rows, :] = theta + pltpu.roll(mom, LANES // 2, 1)
    gath_buf[2, rows, :] = hmat + part_buf[last]
    copies = []
    for off in range(1, n_chip):
        copies.append(
            pltpu.make_async_remote_copy(
                src_ref=gath_buf.at[pl.ds(1, 2), rows, :],
                dst_ref=gath_buf.at[pl.ds(1, 2), rows, :],
                send_sem=fin_send.at[off - 1],
                recv_sem=fin_recv.at[off - 1],
                device_id={"data": lax.rem(chip + off, n_chip) * CORES + core},
                device_id_type=MESH,
            )
        )
    for copy in copies:
        copy.start()
    for copy in copies:
        copy.wait()
    all_out[: LANES, :] = gath_buf[1].T
    all_out[LANES :, :] = gath_buf[2].T[:steps]


def solution(mesh):
    n_dev = mesh.shape["data"]
    n_chip = n_dev // CORES
    row_spec = P("data", None)
    chain_spec = P(None, "parts")

    def local_chains(feat_rows, labels, pos_init, mom_init, step_sizes):
        rows, feats = feat_rows.shape
        chains_all = pos_init.shape[1]
        steps = step_sizes.shape[0]
        chains = chains_all // n_chip
        block_rows = rows // BLOCKS

        vmem = pl.BlockSpec(memory_space=pltpu.VMEM)
        dma = pltpu.SemaphoreType.DMA
        slots = len(ALONE) + CORES * len(SHARED)
        ends = pl.pallas_call(
            functools.partial(chain_kernel, n_dev),
            out_shape=jax.ShapeDtypeStruct((LANES + steps, chains_all), jnp.float32),
            in_specs=[vmem] * 5,
            out_specs=vmem,
            scratch_shapes=[
                pltpu.VMEM((slots, block_rows, BLOCKS * FPAD), jnp.bfloat16),
                pltpu.VMEM((slots, BLOCKS * FPAD, block_rows), jnp.bfloat16),
                pltpu.VMEM((steps + 1, chains, LANES), jnp.float32),
                pltpu.VMEM((2, chains, LANES), jnp.float32),
                pltpu.VMEM((2, chains, LANES), jnp.float32),
                pltpu.VMEM((3, chains_all, LANES), jnp.float32),
                dma((2,)),
                dma((2,)),
                dma((n_chip - 1,)),
                dma((n_chip - 1,)),
                dma((40,)),
                dma((40,)),
                dma((2 * len(SHARED),)),
                dma((2 * len(SHARED),)),
            ],
            compiler_params=pltpu.CompilerParams(
                collective_id=0, has_side_effects=True, vmem_limit_bytes=60 * 1024 * 1024
            ),
        )(feat_rows.T, labels.reshape(rows // LANES, LANES), pos_init, mom_init, step_sizes)
        return ends[:feats], ends[LANES // 2 : LANES // 2 + feats], ends[LANES:]

    return jax.shard_map(local_chains, mesh=mesh, in_specs=(row_spec, P("data"), chain_spec, chain_spec, chain_spec), out_specs=(chain_spec, chain_spec, chain_spec), check_vma=False)
```

time: 278 us -> 268 us (0.964)
  Pallas kernels: 271 us -> 264 us
    pallas_call x1, Pallas kernels: 271 us -> 264 us  [local_chains(): pl.pallas_call(functools.partial(chain_kernel, n_dev), out_shape=jax.Shap...]
where the time goes in v3:
time: 268 us
  Pallas kernels  264 us (99%)
  local copies, waits for them, and re-layouts  2.76 us (1%)
    pallas_call x1, Pallas kernels, local_chains(): pl.pallas_call(functools.partial(chain_kernel, n_dev), out_shape=jax.Shap...  264 us

profile of v3, /device:TPU:97, one launch (start us, length us, event | category | flops | bytes accessed | tf_op | source)
XLA Modules:
  0.0 267.8 jit_solution(13871639982406529295)
XLA Ops:
  0.6 264.4 %shard_map.76 = f32[192,128]{1,0:T(8,128)} custom-call(bf16[54,4096]{1,0:T(8,128)(2,1)} %bitcast.2, s32[32,128]{1,0:T(8,128)} %bitcast.3, f32[54,128]{1,0:T(8,128)} %pos_ref.1, f32[54,128]{1,0:T(8,128)} %mom_ref.1, f32[64,128]{1,0:T(8,128)} %step_ref.1), custom_call_target="tpu_custom_call" | custom-call | tf_op jit(solution)/shard_map/pallas_call | solution.py:433
  265.1 1.4 fusion
  266.5 1.4 slice.11

commit v4 on v3

--- a/solution.py
+++ b/solution.py
@@ -14,8 +14,8 @@
 LANES = 128
 FPAD = 56
 BLOCKS = 16
-UNIT = 8
-MID_LAG, GRAD_LAG, SWAP_LAG = 2, 3, 2
+UNIT = 4
+MID_LAG, GRAD_LAG, SWAP_LAG = 5, 6, 5
 LN2 = 0.6931471805599453
 OFFSETS = [(dx, dy) for dy in (0, -1, 1, 2) for dx in (0, -1, 1, 2)]
 SHARED = [(0, 0), (-1, 0), (1, 0)]
@@ -308,8 +308,6 @@
             h = jnp.tanh(u)
             pos_part = jnp.maximum(u, 0.0)
             fac = 1.0 + jnp.abs(h)
-            pos_part = pos_part[: 4 * chains] + pos_part[4 * chains :]
-            fac = fac[: 4 * chains] * fac[4 * chains :]
             ramp, prod = sums[which]
             sums[which] = (ramp + (pos_part[:, :LANES] + pos_part[:, LANES:]), prod * (fac[:, :LANES] * fac[:, LANES:]))
             return (1.0 + h).astype(jnp.bfloat16)
@@ -319,7 +317,7 @@
             totals[which][strip] = totals[which][strip] + part
 
         def last_strips(which, ks):
-            resid = jnp.concatenate([resids[k, 1][4 * chains :] for k in ks], axis=0)
+            resid = jnp.concatenate([resids[k, 3] for k in ks], axis=0)
             cols = jnp.concatenate([xs[k, :, 3 * 256 :] for k in ks], axis=1)
             if len(ks) == 1:
                 part = jnp.dot(resid, cols, preferred_element_type=jnp.float32)
@@ -329,14 +327,14 @@
             else:
                 add_strip(which, 3, resid, cols)
 
-        def strips_of(k, stage):
+        def strips_of(k, unit):
             which = int(k >= n_alone)
-            if stage == 0:
-                add_strip(which, 0, resids[k, 0][: 6 * chains], xs[k, :, :256])
-                mid = jnp.concatenate([resids[k, 0][4 * chains :], resids[k, 1][: 2 * chains]], axis=0)
-                add_strip(which, 1, mid, xs[k, :, 256:512])
+            if unit == 0:
                 return
-            add_strip(which, 2, resids[k, 1][: 6 * chains], xs[k, :, 512:768])
+            resid = jnp.concatenate([resids[k, unit - 1], resids[k, unit][: 2 * chains]], axis=0)
+            add_strip(which, unit - 1, resid, xs[k, :, (unit - 1) * 256 : unit * 256])
+            if unit < 3:
+                return
             ends = k in (n_alone - 1, n_slots - 1)
             first = 0 if which == 0 else n_alone
             if (k - first) % 2:
@@ -345,17 +343,18 @@
                 last_strips(which, [k])
 
         logits = {}
-        units = 2 * n_slots
+        per = BLOCKS // UNIT
+        units = per * n_slots
         for turn_no in range(units + GRAD_LAG):
             if turn_no < units:
-                logits[turn_no] = logits_of(turn_no // 2, turn_no % 2)
+                logits[turn_no] = logits_of(turn_no // per, turn_no % per)
             job = turn_no - MID_LAG
             if 0 <= job < units:
-                resids[job // 2, job % 2] = resids_of(logits.pop(job), int(job // 2 >= n_alone))
+                resids[job // per, job % per] = resids_of(logits.pop(job), int(job // per >= n_alone))
             job = turn_no - GRAD_LAG
             if job >= 0:
-                strips_of(job // 2, job % 2)
-            if job == 2 * n_alone - 1 + SWAP_LAG:
+                strips_of(job // per, job % per)
+            if job == per * n_alone - 1 + SWAP_LAG:
                 mine = gather_blocks(totals[0])
                 mine_buf[slot] = mine
                 copy.start()

time: 268 us -> 258 us (0.963)
  Pallas kernels: 264 us -> 255 us
    pallas_call x1, Pallas kernels: 264 us -> 255 us  [local_chains(): pl.pallas_call(functools.partial(chain_kernel, n_dev), out_shape=jax.Shap...]
where the time goes in v4:
time: 258 us
  Pallas kernels  255 us (99%)
  local copies, waits for them, and re-layouts  2.76 us (1%)
    pallas_call x1, Pallas kernels, local_chains(): pl.pallas_call(functools.partial(chain_kernel, n_dev), out_shape=jax.Shap...  255 us

profile of v4, /device:TPU:97, one launch (start us, length us, event | category | flops | bytes accessed | tf_op | source)
XLA Modules:
  0.0 258.0 jit_solution(2729265863012207809)
XLA Ops:
  0.6 254.6 %shard_map.76 = f32[192,128]{1,0:T(8,128)} custom-call(bf16[54,4096]{1,0:T(8,128)(2,1)} %bitcast.2, s32[32,128]{1,0:T(8,128)} %bitcast.3, f32[54,128]{1,0:T(8,128)} %pos_ref.1, f32[54,128]{1,0:T(8,128)} %mom_ref.1, f32[64,128]{1,0:T(8,128)} %step_ref.1), custom_call_target="tpu_custom_call" | custom-call | tf_op jit(solution)/shard_map/pallas_call | solution.py:432
  255.2 1.4 fusion
  256.6 1.4 slice.11

commit v5 on v4

--- a/solution.py
+++ b/solution.py
@@ -163,9 +163,9 @@
         buf[...] = own_rows(ref)
         return buf[pl.ds(pl.multiple_of(chip * chains, chains), chains), :]
 
-    theta0 = mine_of(pos_ref, gath_buf.at[0])
-    mom0 = mine_of(mom_ref, gath_buf.at[0])
-    eps_rows = mine_of(step_ref, gath_buf.at[0])
+    theta0 = mine_of(pos_ref, gath_buf.at[3])
+    mom0 = mine_of(mom_ref, gath_buf.at[3])
+    eps_rows = mine_of(step_ref, gath_buf.at[3])
     for l in range(steps):
         eps_buf[l + 1] = jnp.broadcast_to(eps_rows[:, l : l + 1], (chains, LANES))
     eps_buf[0] = jnp.zeros((chains, LANES), jnp.float32)
@@ -377,40 +377,37 @@
     kinetic = jnp.where(low, mom * mom * (0.5 / CORES), 0.0)
     hmat = jnp.where(lane == steps - 1, jnp.sum(carried + kinetic, axis=1, keepdims=True), hmat)
 
-    last = (steps + 1) % 2
-    mine_buf[last] = hmat
-    copy = pltpu.make_async_remote_copy(
-        src_ref=mine_buf.at[last],
-        dst_ref=part_buf.at[last],
-        send_sem=send_sem.at[last],
-        recv_sem=recv_sem.at[last],
-        device_id=partner,
-        device_id_type=MESH,
-    )
-    copy.start()
-    copy.wait()
-
     rows = pl.ds(pl.multiple_of(chip * chains, chains), chains)
-    gath_buf[1, rows, :] = theta + pltpu.roll(mom, LANES // 2, 1)
-    gath_buf[2, rows, :] = hmat + part_buf[last]
+    gath_buf[0, rows, :] = theta + pltpu.roll(mom, LANES // 2, 1)
+    gath_buf[1 + core, rows, :] = hmat
     copies = []
+
+    def spread(plane, device):
+        part = gath_buf.at[plane, rows, :]
+        sems = (fin_send.at[len(copies)], fin_recv.at[len(copies)])
+        copies.append(pltpu.make_async_remote_copy(part, part, *sems, device_id={"data": device}, device_id_type=MESH))
+
     for off in range(1, n_chip):
-        copies.append(
-            pltpu.make_async_remote_copy(
-                src_ref=gath_buf.at[pl.ds(1, 2), rows, :],
-                dst_ref=gath_buf.at[pl.ds(1, 2), rows, :],
-                send_sem=fin_send.at[off - 1],
-                recv_sem=fin_recv.at[off - 1],
-                device_id={"data": lax.rem(chip + off, n_chip) * CORES + core},
-                device_id_type=MESH,
-            )
-        )
+        other = lax.rem(chip + off, n_chip) * CORES
+        spread(0, other + core)
+        spread(1 + core, other + core)
+        spread(1 + core, other + 1 - core)
+    spread(1 + core, chip * CORES + 1 - core)
     for copy in copies:
         copy.start()
     for copy in copies:
-        copy.wait()
-    all_out[: LANES, :] = gath_buf[1].T
-    all_out[LANES :, :] = gath_buf[2].T[:steps]
+        copy.wait_send()
+    arrived = 0
+    for off in range(1, n_chip):
+        origin = pl.ds(pl.multiple_of(lax.rem(chip + n_chip - off, n_chip) * chains, chains), chains)
+        for plane in (0, 1 + core, 2 - core):
+            part = gath_buf.at[plane, origin, :]
+            pltpu.make_async_copy(part, part, fin_recv.at[arrived]).wait()
+            arrived += 1
+    part = gath_buf.at[2 - core, rows, :]
+    pltpu.make_async_copy(part, part, fin_recv.at[arrived]).wait()
+    all_out[: LANES, :] = gath_buf[0].T
+    all_out[LANES :, :] = (gath_buf[1] + gath_buf[2]).T[:steps]
 
 
 def solution(mesh):
@@ -440,11 +437,11 @@
                 pltpu.VMEM((steps + 1, chains, LANES), jnp.float32),
                 pltpu.VMEM((2, chains, LANES), jnp.float32),
                 pltpu.VMEM((2, chains, LANES), jnp.float32),
-                pltpu.VMEM((3, chains_all, LANES), jnp.float32),
+                pltpu.VMEM((4, chains_all, LANES), jnp.float32),
                 dma((2,)),
                 dma((2,)),
-                dma((n_chip - 1,)),
-                dma((n_chip - 1,)),
+                dma((3 * n_chip - 2,)),
+                dma((3 * n_chip - 2,)),
                 dma((40,)),
                 dma((40,)),
                 dma((2 * len(SHARED),)),

time: 258 us -> 259 us (level)
  no operation moved by 1% of the time
where the time goes in v5:
time: 259 us; the launch traced here: 258 us
  Pallas kernels  255 us (98%)
  local copies, waits for them, and re-layouts  2.76 us (1%)
    pallas_call x1, Pallas kernels, local_chains(): pl.pallas_call(functools.partial(chain_kernel, n_dev), out_shape=jax.Shap...  255 us

profile of v5, /device:TPU:97, one launch (start us, length us, event | category | flops | bytes accessed | tf_op | source)
XLA Modules:
  0.0 258.4 jit_solution(11738628162489680183)
XLA Ops:
  0.6 255.0 %shard_map.76 = f32[192,128]{1,0:T(8,128)} custom-call(bf16[54,4096]{1,0:T(8,128)(2,1)} %bitcast.2, s32[32,128]{1,0:T(8,128)} %bitcast.3, f32[54,128]{1,0:T(8,128)} %pos_ref.1, f32[54,128]{1,0:T(8,128)} %mom_ref.1, f32[64,128]{1,0:T(8,128)} %step_ref.1), custom_call_target="tpu_custom_call" | custom-call | tf_op jit(solution)/shard_map/pallas_call | solution.py:429
  255.6 1.4 fusion
  257.0 1.4 slice.11
